TPU v7x, 256 devices: a whole 4x4x8 slice. The times are simulated.
256 devices in a mesh: dev: 128 (over y, x, z), rep: 2 (over core).
Axes of the slice: x: 4, y: 4, z: 8, core: 2. Of those that a mesh axis runs over, the one named last changes fastest.
Arguments:
- embeddings: float32 [32768, 4096], P(('rep', 'dev')), parts along dimension 0, may hold values from -130 to 130
- cluster_id: int32 [32768], P(('rep', 'dev')), parts along dimension 0, may hold values from 0 to 255, as said below
- member_order: int32 [32768], P(('rep', 'dev')), parts along dimension 0, may hold values from 0 to 127, as said below
- cluster_slot: int32 [512], P('rep'), parts along dimension 0, may hold values from 0 to 255, each once
- cluster_size: int32 [512], P('rep'), parts along dimension 0, may hold values from 16 to 128, as said below
Outputs:
- best_similarity: float32 [32768], P(('rep', 'dev')), parts along dimension 0
- keep: int32 [32768], P(('rep', 'dev')), parts along dimension 0
- cluster_mean: float32 [512], P(('rep', 'dev')), parts along dimension 0
There are 2 independent parts, one for each index of `rep`. A program takes and returns all parts, laid end to end along the dimension named above; each array names one. Nothing has to cross between parts.
Inputs may be any that keep to these rules, and one draw needn't show every extreme that they name: `cluster_id`: every cluster holds at most 128 rows and some cluster exactly 128. A cluster of n members has floor(n / 128) or ceil(n / 128) of them among the rows of each device, so at most 1, a number reached on every device. `member_order`: within a cluster of n members the ranks are 0 to n - 1, each once. `cluster_slot`: a permutation; cluster c is owned by device cluster_slot[c] // 2 of dev. `cluster_size`: the number of rows whose cluster_id is c.
All inputs are finite; a program needn't handle non-finite values.
Results may differ from a plain program's by a relative error of at most 0.0003.
Values may be sent and summed in bfloat16 or wider, within the bound.
No kernel may reach another device: no remote copies, remote signals or barrier semaphores. Data moves between devices by JAX's collectives and lax.ppermute only.
A program may use at most 64 MiB of HBM per device.

v0:
```python
import jax
import jax.numpy as jnp
from jax import lax
from jax.sharding import PartitionSpec as P

CAP = 128


norm_eps = 1e-06
cutoff = 0.8


def normalized(values):
    squares_sum = jnp.sum(values * values, axis=1, keepdims=True)
    return (values * lax.rsqrt(squares_sum + norm_eps)).astype(jnp.bfloat16)


def block_best(row_units, col_units, is_live):
    similar = jnp.einsum("cid,cjd->cij", row_units, col_units, preferred_element_type=jnp.float32)
    count_rows = row_units.shape[1]
    count_cols = col_units.shape[1]
    row_pos = lax.broadcasted_iota(jnp.int32, (count_rows, count_cols), 0)
    col_pos = lax.broadcasted_iota(jnp.int32, (count_rows, count_cols), 1)
    allowed = (col_pos < row_pos)[None] & is_live[:, None, :count_cols]
    return jnp.max(jnp.where(allowed, similar, -1.0), axis=2)


def body(embeddings, cluster_id, member_order, cluster_slot, cluster_size):
    devices = lax.axis_size("dev")
    clusters = cluster_slot.shape[0]
    per_owner = clusters // devices
    row_count = embeddings.shape[0]
    capacity = CAP
    per_pair = capacity // devices
    columns = lax.broadcasted_iota(jnp.int32, (row_count, clusters), 1)
    member = cluster_id[:, None] == columns
    slot_row = jnp.sum(jnp.where(member, cluster_slot[None, :], 0), axis=1)
    earlier = (
        lax.broadcasted_iota(jnp.int32, (row_count, row_count), 1)
        < lax.broadcasted_iota(jnp.int32, (row_count, row_count), 0)
    ).astype(jnp.bfloat16)
    before = jnp.dot(earlier, member.astype(jnp.bfloat16), preferred_element_type=jnp.float32)
    row_rank = jnp.sum(jnp.where(member, before, 0.0), axis=1).astype(jnp.int32)
    send_place = slot_row * per_pair + row_rank
    source_row = (
        jnp.zeros((clusters * per_pair,), jnp.int32)
        .at[send_place]
        .set(jnp.arange(row_count, dtype=jnp.int32) + 1)
    )
    filled = source_row > 0
    row_pick = jnp.maximum(source_row - 1, 0)
    sent_order = jnp.where(filled, member_order[row_pick], -1)
    payload = normalized(embeddings)[row_pick]
    got_rows, got_order = (
        lax.all_to_all(payload, "dev", split_axis=0, concat_axis=0, tiled=True),
        lax.all_to_all(sent_order, "dev", split_axis=0, concat_axis=0, tiled=True),
    )
    slots_in = got_order.shape[0]
    local_cluster = jnp.arange(slots_in, dtype=jnp.int32) // per_pair % per_owner
    is_valid = got_order >= 0
    position = jnp.where(is_valid, local_cluster * capacity + got_order, per_owner * capacity)
    arrival = (
        jnp.zeros((per_owner * capacity,), jnp.int32)
        .at[position]
        .set(jnp.arange(slots_in, dtype=jnp.int32) + 1, mode="drop")
    )
    occupied = arrival > 0
    gathered = got_rows[jnp.maximum(arrival - 1, 0)]
    unit_rows = jnp.where(occupied[:, None], gathered, jnp.zeros((), jnp.bfloat16))
    unit_rows = unit_rows.reshape(per_owner, capacity, unit_rows.shape[1])
    owner_index = lax.axis_index("dev")
    my_slots = owner_index * per_owner + jnp.arange(per_owner, dtype=jnp.int32)
    own_match = cluster_slot[None, :] == my_slots[:, None]
    my_size = jnp.sum(jnp.where(own_match, cluster_size[None, :], 0), axis=1)
    spot_index = lax.broadcasted_iota(jnp.int32, (per_owner, capacity), 1)
    is_live = occupied.reshape(per_owner, capacity) & (spot_index < my_size[:, None])
    nearest = block_best(unit_rows, unit_rows, is_live)
    best_spot = jnp.where(is_live, nearest, -1.0)
    cluster_mean = jnp.sum(jnp.where(is_live, best_spot, 0.0), axis=1) / my_size.astype(jnp.float32)
    flat_best = best_spot.reshape(-1)
    answer = jnp.where(is_valid, flat_best[jnp.minimum(position, per_owner * capacity - 1)], 0.0)
    returned = lax.all_to_all(answer, "dev", split_axis=0, concat_axis=0, tiled=True)
    row_best = returned[send_place]
    keep_mask = (row_best < cutoff).astype(jnp.int32)
    return (row_best, keep_mask, cluster_mean)


def solution(mesh):
    placed = (P(("rep", "dev"), None), P(("rep", "dev")), P(("rep", "dev")), P("rep"), P("rep"))
    return jax.shard_map(
        body,
        mesh=mesh,
        in_specs=placed,
        out_specs=(P(("rep", "dev")), P(("rep", "dev")), P(("rep", "dev"))),
        check_vma=False,
    )
```

profile of v0, /device:TPU:2, one launch (start us, length us, event | category | flops | bytes accessed | tf_op | source)
XLA Modules:
  0.0 128.7 jit_solution(10026192653915958630)
XLA Ops:
  0.7 1.1 fusion.6
  1.8 0.9 select_reduce_fusion
  2.7 1.0 scatter_custom_fusion
  3.7 1.9 %gather_fusion = s32[256]{0:T(256)S(1)} fusion(s32[128]{0:T(128)S(1)} %copy-done, s32[1024]{0:T(1024)S(1)} %pad_clamp_fusion.3), kind=kCustom, calls=%fused_computation | custom fusion | bytes 3072 | tf_op jit(solution)/shard_map/gather | solution.py:52
  5.6 0.8 all_to_all.22
  6.4 15.4 %all-to-all-start = ((s32[128,2,1]{1,2,0:T(1,128)}), s32[128,2,1]{1,2,0:T(1,128)S(1)}, u32[]{:S(2)}, u32[]{:S(2)}) async-start(s32[128,2,1]{1,2,0:T(1,128)} %bitcast.2), calls=%async_computation | async-start | bytes 131072 | tf_op jit(solution)/shard_map/all_to_all | solution.py:56
  21.8 1.8 %multiply_reduce_fusion = f32[128]{0:T(128)S(1)} fusion(f32[128,4096]{1,0:T(8,128)} %param.5), kind=kLoop, calls=%fused_computation.10 | loop fusion | flops 1048448 | bytes 2097664 | tf_op jit(solution)/shard_map/reduce_sum | solution.py:14
  23.9 1.8 %gather_fusion.1 = bf16[256,4096]{1,0:T(8,128)(2,1)S(1)} fusion(bf16[128,4096]{1,0:T(8,128)(2,1)S(1)} %multiply_convert_fusion, s32[1024]{0:T(1024)S(1)} %pad_clamp_fusion.3), kind=kCustom, calls=%fused_computation.1 | custom fusion | bytes 4195328 | tf_op jit(solution)/shard_map/gather | solution.py:53
  25.7 2.7 %all_to_all.25 = bf16[128,2,4096]{2,1,0:T(2,128)(2,1)} reshape(bf16[256,4096]{1,0:T(8,128)(2,1)S(1)} %gather_fusion.1) | data formatting | bytes 4194304 | tf_op jit(solution)/shard_map/all_to_all | solution.py:55
  28.4 4.5 %all-to-all-done = s32[128,2,1]{1,2,0:T(1,128)S(1)} async-done(((s32[128,2,1]{1,2,0:T(1,128)}), s32[128,2,1]{1,2,0:T(1,128)S(1)}, u32[]{:S(2)}, u32[]{:S(2)}) %all-to-all-start) | async-done | bytes 1056 | tf_op jit(solution)/shard_map/all_to_all | solution.py:56
  32.9 9.9 %all-to-all-start.1 = ((bf16[128,2,4096]{2,1,0:T(2,128)(2,1)}), bf16[128,2,4096]{2,1,0:T(2,128)(2,1)}, u32[]{:S(2)}, u32[]{:S(2)}) async-start(bf16[128,2,4096]{2,1,0:T(2,128)(2,1)} %all_to_all.25), calls=%async_computation.1 | async-start | bytes 4194304 | tf_op jit(solution)/shard_map/all_to_all | solution.py:55
  43.6 0.8 reduce.6
  44.6 1.4 %scatter_custom_fusion.1 = s32[256]{0:T(256)S(1)} fusion(s32[256]{0:T(256)S(1)} %bitcast.24, s32[256]{0:T(256)S(1)} %iota_add_fusion, s32[]{:T(128)} %constant.27.clone.1), kind=kCustom, calls=%fused_computation.52 | custom fusion | bytes 1028 | tf_op jit(solution)/shard_map/scatter | solution.py:65
  46.1 47.2 %all-to-all-done.1 = bf16[128,2,4096]{2,1,0:T(2,128)(2,1)} async-done(((bf16[128,2,4096]{2,1,0:T(2,128)(2,1)}), bf16[128,2,4096]{2,1,0:T(2,128)(2,1)}, u32[]{:S(2)}, u32[]{:S(2)}) %all-to-all-start.1) | async-done | bytes 2097184 | tf_op jit(solution)/shard_map/all_to_all | solution.py:55
  93.2 2.7 %all_to_all.27 = bf16[256,4096]{1,0:T(8,128)(2,1)S(1)} reshape(bf16[128,2,4096]{2,1,0:T(2,128)(2,1)} %all-to-all-done.1) | data formatting | bytes 4194304 | tf_op jit(solution)/shard_map/all_to_all | solution.py:55
  96.0 3.2 %gather_fusion.2 = bf16[256,4096]{1,0:T(8,128)(2,1)} fusion(bf16[256,4096]{1,0:T(8,128)(2,1)S(1)} %all_to_all.27, s32[1024]{0:T(1024)S(1)} %pad_clamp_fusion.2), kind=kCustom, calls=%fused_computation.2 | custom fusion | bytes 4195328 | tf_op jit(solution)/shard_map/gather | solution.py:68
  99.2 3.0 %fusion.7 = f32[2,128]{1,0:T(2,128)S(1)} fusion(bf16[2,128,4096]{2,1,0:T(8,128)(2,1)} %bitcast.21, pred[2,128]{1,0:T(4,128)(4,1)S(1)} %get-tuple-element.6, pred[2,128]{1,0:T(4,128)(4,1)S(1)} %get-tuple-element.5, pred[128,128]{0,1:T(8,128)(4,1)S(1)} %iota_compare_fusion.2), kind=kOutput, calls=%fused_computation.15 | convolution fusion | flops 269582080 | bytes 2115072 | tf_op jit(solution)/shard_map/cid,cjd->cij/dot_general | solution.py:19
  102.4 2.0 %gather_fusion.3 = f32[256]{0:T(256)S(1)} fusion(f32[256]{0:T(256)S(1)} %fusion.13, s32[1024]{0:T(1024)S(1)} %pad_clamp_fusion.1), kind=kCustom, calls=%fused_computation.3 | custom fusion | bytes 3072 | tf_op jit(solution)/shard_map/gather | solution.py:81
  104.5 0.6 compare_select_fusion
  105.1 9.1 %all-to-all-start.2 = ((f32[128,2,1]{1,2,0:T(1,128)}), f32[128,2,1]{1,2,0:T(1,128)S(1)}, u32[]{:S(2)}, u32[]{:S(2)}) async-start(f32[128,2,1]{1,2,0:T(1,128)} %bitcast.10), calls=%async_computation.2 | async-start | bytes 131072 | tf_op jit(solution)/shard_map/all_to_all | solution.py:82
  114.3 0.5 convert_divide_fusion
  114.8 10.6 %all-to-all-done.2 = f32[128,2,1]{1,2,0:T(1,128)S(1)} async-done(((f32[128,2,1]{1,2,0:T(1,128)}), f32[128,2,1]{1,2,0:T(1,128)S(1)}, u32[]{:S(2)}, u32[]{:S(2)}) %all-to-all-start.2) | async-done | bytes 1056 | tf_op jit(solution)/shard_map/all_to_all | solution.py:82
  125.9 0.8 reduce.7
  126.9 1.3 gather_fusion.4
  (36 shorter events, 2.7 us)
Async XLA Ops:
  0.6 3.1 %copy-start = (s32[128]{0:T(128)S(1)}, s32[128]{0:T(128)}, u32[]{:S(2)}) copy-start(s32[128]{0:T(128)} %param.7) | copy-start | bytes 1540
  0.6 23.0 %copy-start.1 = (f32[128,4096]{1,0:T(8,128)S(1)}, f32[128,4096]{1,0:T(8,128)}, u32[]{:S(2)}) copy-start(f32[128,4096]{1,0:T(8,128)} %param.5) | copy-start | bytes 6291460
  6.4 26.5 %all-to-all-start = ((s32[128,2,1]{1,2,0:T(1,128)}), s32[128,2,1]{1,2,0:T(1,128)S(1)}, u32[]{:S(2)}, u32[]{:S(2)}) async-start(s32[128,2,1]{1,2,0:T(1,128)} %bitcast.2), calls=%async_computation | async-start | bytes 131072 | tf_op jit(solution)/shard_map/all_to_all | solution.py:56
  28.4 14.5 %copy-start.2 = (s32[256]{0:T(256)S(1)}, s32[256]{0:T(256)}, u32[]{:S(2)}) copy-start(s32[256]{0:T(256)} %param.8) | copy-start | bytes 3076
  28.4 14.5 %copy-start.3 = (s32[256]{0:T(256)S(1)}, s32[256]{0:T(256)}, u32[]{:S(2)}) copy-start(s32[256]{0:T(256)} %param.9) | copy-start | bytes 3076
  32.9 60.3 %all-to-all-start.1 = ((bf16[128,2,4096]{2,1,0:T(2,128)(2,1)}), bf16[128,2,4096]{2,1,0:T(2,128)(2,1)}, u32[]{:S(2)}, u32[]{:S(2)}) async-start(bf16[128,2,4096]{2,1,0:T(2,128)(2,1)} %all_to_all.25), calls=%async_computation.1 | async-start | bytes 4194304 | tf_op jit(solution)/shard_map/all_to_all | solution.py:55
  105.1 20.3 %all-to-all-start.2 = ((f32[128,2,1]{1,2,0:T(1,128)}), f32[128,2,1]{1,2,0:T(1,128)S(1)}, u32[]{:S(2)}, u32[]{:S(2)}) async-start(f32[128,2,1]{1,2,0:T(1,128)} %bitcast.10), calls=%async_computation.2 | async-start | bytes 131072 | tf_op jit(solution)/shard_map/all_to_all | solution.py:82
  128.2 0.5 copy-start.4
where the time goes:
time: 129 us
  waiting for transfers between devices  62.3 us (48%)
  starting transfers between devices  34.5 us (27%)
  local copies, waits for them, and re-layouts  20.1 us (16%)
  other arithmetic  6.7 us (5%)
  matrix products  4.16 us (3%)
    all_to_all x1, waiting for transfers between devices, body(): lax.all_to_all(payload, 'dev', split_axis=0, concat_axis=0, tiled=True)  47.2 us
    all_to_all x1, starting transfers between devices, body(): lax.all_to_all(sent_order, 'dev', split_axis=0, concat_axis=0, tiled=True)  15.4 us
    all_to_all x1, waiting for transfers between devices, body(): lax.all_to_all(answer, 'dev', split_axis=0, concat_axis=0, tiled=True)  10.6 us
    all_to_all x1, starting transfers between devices, body(): lax.all_to_all(payload, 'dev', split_axis=0, concat_axis=0, tiled=True)  9.9 us
    all_to_all x1, starting transfers between devices, body(): lax.all_to_all(answer, 'dev', split_axis=0, concat_axis=0, tiled=True)  9.14 us
    all_to_all x2, local copies, waits for them, and re-layouts, body(): lax.all_to_all(payload, 'dev', split_axis=0, concat_axis=0, tiled=True)  5.4 us
    all_to_all x1, waiting for transfers between devices, body(): lax.all_to_all(sent_order, 'dev', split_axis=0, concat_axis=0, tiled=True)  4.51 us
    gather x1, local copies, waits for them, and re-layouts, body(): gathered = got_rows[jnp.maximum(arrival - 1, 0)]  3.2 us
  transfers between devices with their start and end apart: 3, of which 3 were waited for; matrix products, arithmetic and copies ran while one was open for 6% of the time, Pallas kernels for 0%

commit v1 on v0

v1 whole, which is shorter than its diff:
```python
import jax
import jax.numpy as jnp
from jax import lax
from jax.experimental import pallas as pl
from jax.experimental.pallas import tpu as pltpu
from jax.sharding import PartitionSpec as P

CAP = 128
LANES = 128

norm_eps = 1e-06
cutoff = 0.8


def iota(shape, axis):
    return lax.broadcasted_iota(jnp.int32, shape, axis)


def table_lookup(cluster_row, table_row):
    clusters = table_row.shape[1]
    hit = (iota((clusters, cluster_row.shape[1]), 0) == cluster_row).astype(jnp.bfloat16)
    table = jnp.broadcast_to(table_row.astype(jnp.bfloat16), (8, clusters))
    return jnp.dot(table, hit, preferred_element_type=jnp.float32)[:1]


def place_kernel(emb_ref, id_ref, order_ref, slot_ref, size_ref, out_ref, where_ref):
    values = emb_ref[...]
    squares_sum = jnp.sum(values * values, axis=1, keepdims=True)
    unit = (values * lax.rsqrt(squares_sum + norm_eps)).astype(jnp.bfloat16)
    ids = id_ref[...]
    slot_of = table_lookup(ids, slot_ref[...]).astype(jnp.int32)
    size_of = table_lookup(ids, size_ref[...]).astype(jnp.int32)
    order = order_ref[...]
    code = jnp.where(order < size_of, order + 1, 0).astype(jnp.float32)
    slots = out_ref.shape[0]
    depth = values.shape[1]
    hit = iota((slots, values.shape[0]), 0) == slot_of
    out_ref[:, :depth] = jnp.dot(
        hit.astype(jnp.bfloat16), unit, preferred_element_type=jnp.float32
    ).astype(jnp.bfloat16)
    rank = jnp.sum(jnp.where(hit, code, 0.0), axis=1, keepdims=True)
    out_ref[:, depth:] = jnp.broadcast_to(rank, (slots, LANES)).astype(jnp.bfloat16)
    where_ref[...] = slot_of


def best_kernel(got_ref, slot_ref, size_ref, best_ref, mean_ref, spread_ref):
    rows = got_ref.shape[0]
    depth = got_ref.shape[1] - LANES
    unit = got_ref[:, :depth]
    coded = got_ref[:, depth:]
    similar = lax.dot_general(
        unit, unit, (((1,), (1,)), ((), ())), preferred_element_type=jnp.float32
    )
    rank_col = coded.astype(jnp.float32)[:, :1]
    first = (iota((8, LANES), 1) == 0).astype(jnp.bfloat16)
    rank_row = lax.dot_general(
        first, coded, (((1,), (1,)), ((), ())), preferred_element_type=jnp.float32
    )[:1]
    same = ((iota((rows, rows), 0) ^ iota((rows, rows), 1)) & 1) == 0
    allowed = same & (rank_row > 0.0) & (rank_row < rank_col)
    best = jnp.max(jnp.where(allowed, similar, -1.0), axis=1, keepdims=True)
    spread_ref[...] = jnp.broadcast_to(best, spread_ref.shape)
    live_col = jnp.broadcast_to(rank_col, spread_ref.shape) > 0.0
    summed = jnp.where(live_col, spread_ref[...], 0.0)
    odd = (iota(spread_ref.shape, 0) & 1) == 1
    lane = iota((1, LANES), 1)
    total = jnp.where(
        lane == 0,
        jnp.sum(jnp.where(odd, 0.0, summed), axis=0, keepdims=True),
        jnp.sum(jnp.where(odd, summed, 0.0), axis=0, keepdims=True),
    )
    half = rows // 2
    even_best = spread_ref[pl.ds(0, half, stride=2), :]
    odd_best = spread_ref[pl.ds(1, half, stride=2), :]
    best_ref[...] = jnp.where(iota((half, LANES), 1) == 0, even_best, odd_best)
    first_slot = lax.axis_index("dev") * 2
    slots = slot_ref[...]
    sizes = size_ref[...]
    size0 = jnp.sum(jnp.where(slots == first_slot, sizes, 0), axis=1, keepdims=True)
    size1 = jnp.sum(jnp.where(slots == first_slot + 1, sizes, 0), axis=1, keepdims=True)
    size = jnp.where(lane == 0, size0, size1)
    mean_ref[...] = total / size.astype(jnp.float32)


def pick_kernel(back_ref, where_ref, best_ref, keep_ref):
    slot_of = where_ref[...]
    back = back_ref[...]
    owners = iota((back.shape[0], slot_of.shape[1]), 0)
    from_even = jnp.where(owners * 2 == slot_of, back[:, :1], 0.0)
    from_odd = jnp.where(owners * 2 + 1 == slot_of, back[:, 1:2], 0.0)
    best = jnp.sum(from_even + from_odd, axis=0, keepdims=True)
    best_ref[...] = best
    keep_ref[...] = (best < cutoff).astype(jnp.int32)


def body(embeddings, cluster_id, member_order, cluster_slot, cluster_size):
    devices = lax.axis_size("dev")
    rows, depth = embeddings.shape
    clusters = cluster_slot.shape[0]
    ids = cluster_id.reshape(1, rows)
    order = member_order.reshape(1, rows)
    slot = cluster_slot.reshape(1, clusters)
    size = cluster_size.reshape(1, clusters)
    width = depth + LANES
    payload, place = pl.pallas_call(
        place_kernel,
        out_shape=(
            jax.ShapeDtypeStruct((clusters, width), jnp.bfloat16),
            jax.ShapeDtypeStruct((1, rows), jnp.int32),
        ),
        name="place",
    )(embeddings, ids, order, slot, size)
    got = lax.all_to_all(payload, "dev", split_axis=0, concat_axis=0, tiled=True)
    best, mean = pl.pallas_call(
        best_kernel,
        out_shape=(
            jax.ShapeDtypeStruct((devices, LANES), jnp.float32),
            jax.ShapeDtypeStruct((1, LANES), jnp.float32),
        ),
        scratch_shapes=[pltpu.VMEM((clusters, LANES), jnp.float32)],
        name="best",
    )(got, slot, size)
    back = lax.all_to_all(
        best.reshape(devices, 1, LANES), "dev", split_axis=0, concat_axis=0, tiled=True
    ).reshape(devices, LANES)
    row_best, keep = pl.pallas_call(
        pick_kernel,
        out_shape=(
            jax.ShapeDtypeStruct((1, rows), jnp.float32),
            jax.ShapeDtypeStruct((1, rows), jnp.int32),
        ),
        name="pick",
    )(back, place)
    return (row_best.reshape(rows), keep.reshape(rows), mean[0, :2])


def solution(mesh):
    placed = (P(("rep", "dev"), None), P(("rep", "dev")), P(("rep", "dev")), P("rep"), P("rep"))
    return jax.shard_map(
        body,
        mesh=mesh,
        in_specs=placed,
        out_specs=(P(("rep", "dev")), P(("rep", "dev")), P(("rep", "dev"))),
        check_vma=False,
    )
```

time: 129 us -> 105 us (0.81)
  blocking collectives: 0 us -> 68.1 us
  waiting for transfers between devices: 62.3 us -> 9.98 us
  starting transfers between devices: 34.5 us -> 9.07 us
  local copies, waits for them, and re-layouts: 20.1 us -> 8.68 us
  Pallas kernels: 0 us -> 8.55 us
  other arithmetic: 6.7 us -> 0 us
  matrix products: 4.16 us -> 0 us
    all_to_all x0 -> x1, blocking collectives: none -> 68.1 us  [body(): lax.all_to_all(payload, 'dev', split_axis=0, concat_axis=0, tiled=True)]
    all_to_all x3 -> x1, waiting for transfers between devices: 62.3 us -> 9.98 us  [body(): lax.all_to_all(best.reshape(devices, 1, LANES), 'dev', split_axis=0, conc...]
    all_to_all x3 -> x1, starting transfers between devices: 34.5 us -> 9.07 us  [body(): lax.all_to_all(best.reshape(devices, 1, LANES), 'dev', split_axis=0, conc...]
    gather x6 -> x0, local copies, waits for them, and re-layouts: 10.3 us -> none  [the longest x1 3.2 us: body(): gathered = got_rows[jnp.maximum(arrival - 1, 0)]]
    pallas_call x0 -> x3, Pallas kernels: none -> 8.55 us  [the longest x1 3.92 us: body(): pl.pallas_call(place_kernel, out_shape=(jax.ShapeDtypeStruct((clusters, w...]
    dot_general x2 -> x0, matrix products: 4.16 us -> none  [the longest x1 3.02 us: block_best(): jnp.einsum('cid,cjd->cij', row_units, col_units, preferred_element_type=j...]
    reduce_sum x4 -> x0, other arithmetic: 2.98 us -> none  [the longest x1 1.82 us: normalized(): squares_sum = jnp.sum(values * values, axis=1, keepdims=True)]
    scatter x2 -> x0, local copies, waits for them, and re-layouts: 2.37 us -> none  [the longest x1 1.4 us: body(): arrival = jnp.zeros((per_owner * capacity,), jnp.int32).at[position].set(...]
  transfers between devices with their start and end apart: 3 -> 1, of which waited for: 3 -> 1; matrix products, arithmetic and copies ran while one was open for 6% -> 1% of each run, Pallas kernels for 0% -> 0%
where the time goes in v1:
time: 105 us
  blocking collectives  68.1 us (65%)
  waiting for transfers between devices  9.98 us (10%)
  starting transfers between devices  9.07 us (9%)
  local copies, waits for them, and re-layouts  8.68 us (8%)
  Pallas kernels  8.55 us (8%)
    all_to_all x1, blocking collectives, body(): lax.all_to_all(payload, 'dev', split_axis=0, concat_axis=0, tiled=True)  68.1 us
    all_to_all x1, waiting for transfers between devices, body(): lax.all_to_all(best.reshape(devices, 1, LANES), 'dev', split_axis=0, conc...  9.98 us
    all_to_all x1, starting transfers between devices, body(): lax.all_to_all(best.reshape(devices, 1, LANES), 'dev', split_axis=0, conc...  9.07 us
    all_to_all x2, local copies, waits for them, and re-layouts, body(): lax.all_to_all(payload, 'dev', split_axis=0, concat_axis=0, tiled=True)  6.9 us
    pallas_call x1, Pallas kernels, body(): pl.pallas_call(place_kernel, out_shape=(jax.ShapeDtypeStruct((clusters, w...  3.92 us
    pallas_call x1, Pallas kernels, body(): pl.pallas_call(best_kernel, out_shape=(jax.ShapeDtypeStruct((devices, LAN...  3.16 us
  transfers between devices with their start and end apart: 1, of which 1 were waited for; matrix products, arithmetic and copies ran while one was open for 1% of the time, Pallas kernels for 0%

profile of v1, /device:TPU:2, one launch (start us, length us, event | category | flops | bytes accessed | tf_op | source)
XLA Modules:
  0.0 105.1 jit_solution(5339716115933933372)
XLA Ops:
  0.6 3.9 %place.1 = (bf16[256,4224]{1,0:T(8,128)(2,1)}, s32[1,128]{1,0:T(1,128)}) custom-call(f32[128,4096]{1,0:T(8,128)} %emb_ref.1, s32[1,128]{1,0:T(1,128)} %bitcast.18, s32[1,128]{1,0:T(1,128)} %bitcast.19, s32[1,256]{1,0:T(1,128)} %bitcast.14, s32[1,256]{1,0:T(1,128)} %bitcast.16), custom_call_target="tpu_custom_call" | custom-call | tf_op jit(solution)/shard_map/place/pallas_call | solution.py:105
  4.6 2.8 %all_to_all.10 = bf16[128,2,4224]{2,1,0:T(2,128)(2,1)S(1)} reshape(bf16[256,4224]{1,0:T(8,128)(2,1)} %get-tuple-element.9) | data formatting | bytes 4325376 | tf_op jit(solution)/shard_map/all_to_all | solution.py:113
  7.3 68.1 %all_to_all.16 = bf16[128,2,4224]{2,1,0:T(2,128)(2,1)} all-to-all(bf16[128,2,4224]{2,1,0:T(2,128)(2,1)S(1)} %all_to_all.10), channel_id=1, replica_groups=mesh['dev'=128,'rep'=2] {'dev'}, dimensions={0} | all-to-all | bytes 4325376 | tf_op jit(solution)/shard_map/all_to_all | solution.py:113
  75.5 4.1 %all_to_all.12.got_ref = bf16[256,4224]{1,0:T(8,128)(2,1)} reshape(bf16[128,2,4224]{2,1,0:T(2,128)(2,1)} %all_to_all.16) | data formatting | bytes 4325376 | tf_op jit(solution)/shard_map/all_to_all | solution.py:113
  79.6 3.2 %best.1 = (f32[128,128]{1,0:T(8,128)}, f32[1,128]{1,0:T(1,128)}) custom-call(bf16[256,4224]{1,0:T(8,128)(2,1)} %all_to_all.12.got_ref, s32[1,256]{1,0:T(1,128)} %bitcast.15, s32[1,256]{1,0:T(1,128)} %bitcast.17), custom_call_target="tpu_custom_call" | custom-call | tf_op jit(solution)/shard_map/best/pallas_call | solution.py:114
  82.8 9.1 %all-to-all-start.1 = ((f32[128,1,128]{2,1,0:T(1,128)}), f32[128,1,128]{2,1,0:T(1,128)S(1)}, u32[]{:S(2)}, u32[]{:S(2)}) async-start(f32[128,1,128]{2,1,0:T(1,128)} %bitcast.13), calls=%async_computation.1 | async-start | bytes 131072 | tf_op jit(solution)/shard_map/all_to_all | solution.py:123
  91.8 1.2 %slice_bitcast_fusion = f32[2]{0:T(128)} fusion(f32[1,128]{1,0:T(1,128)} %get-tuple-element.14), kind=kLoop, calls=%fused_computation | loop fusion | bytes 16 | tf_op jit(solution)/shard_map/squeeze | solution.py:134
  93.0 10.0 %all-to-all-done.1 = f32[128,1,128]{2,1,0:T(1,128)S(1)} async-done(((f32[128,1,128]{2,1,0:T(1,128)}), f32[128,1,128]{2,1,0:T(1,128)S(1)}, u32[]{:S(2)}, u32[]{:S(2)}) %all-to-all-start.1) | async-done | bytes 65568 | tf_op jit(solution)/shard_map/all_to_all | solution.py:123
  103.0 0.0 copy-start
  103.0 0.6 copy-done
  103.6 1.5 %pick.1 = (f32[1,128]{1,0:T(1,128)}, s32[1,128]{1,0:T(1,128)}) custom-call(f32[128,128]{1,0:T(8,128)} %bitcast.12, s32[1,128]{1,0:T(1,128)} %get-tuple-element.11.where_ref), custom_call_target="tpu_custom_call" | custom-call | tf_op jit(solution)/shard_map/pick/pallas_call | solution.py:126
Async XLA Ops:
  82.8 20.2 %all-to-all-start.1 = ((f32[128,1,128]{2,1,0:T(1,128)}), f32[128,1,128]{2,1,0:T(1,128)S(1)}, u32[]{:S(2)}, u32[]{:S(2)}) async-start(f32[128,1,128]{2,1,0:T(1,128)} %bitcast.13), calls=%async_computation.1 | async-start | bytes 131072 | tf_op jit(solution)/shard_map/all_to_all | solution.py:123
  103.0 0.6 copy-start

commit v2 on v1

--- a/solution.py
+++ b/solution.py
@@ -109,6 +109,7 @@
             jax.ShapeDtypeStruct((1, rows), jnp.int32),
         ),
         name="place",
+        compiler_params=pltpu.CompilerParams(vmem_limit_bytes=24 * 2**20),
     )(embeddings, ids, order, slot, size)
     got = lax.all_to_all(payload, "dev", split_axis=0, concat_axis=0, tiled=True)
     best, mean = pl.pallas_call(
@@ -119,6 +120,7 @@
         ),
         scratch_shapes=[pltpu.VMEM((clusters, LANES), jnp.float32)],
         name="best",
+        compiler_params=pltpu.CompilerParams(vmem_limit_bytes=24 * 2**20),
     )(got, slot, size)
     back = lax.all_to_all(
         best.reshape(devices, 1, LANES), "dev", split_axis=0, concat_axis=0, tiled=True
@@ -130,6 +132,7 @@
             jax.ShapeDtypeStruct((1, rows), jnp.int32),
         ),
         name="pick",
+        compiler_params=pltpu.CompilerParams(vmem_limit_bytes=24 * 2**20),
     )(back, place)
     return (row_best.reshape(rows), keep.reshape(rows), mean[0, :2])
 

time: 105 us -> 102 us (0.971)
  Pallas kernels: 8.55 us -> 3.08 us
  local copies, waits for them, and re-layouts: 8.68 us -> 9.83 us
    unnamed x2 -> x14, local copies, waits for them, and re-layouts: 0.62 us -> 4.26 us
    pallas_call x1, Pallas kernels: 3.92 us -> 0.92 us  [body(): pl.pallas_call(place_kernel, out_shape=(jax.ShapeDtypeStruct((clusters, w...]
    all_to_all x2, local copies, waits for them, and re-layouts: 6.9 us -> 5.06 us  [body(): lax.all_to_all(payload, 'dev', split_axis=0, concat_axis=0, tiled=True)]
    pallas_call x1, Pallas kernels: 3.16 us -> 1.53 us  [body(): pl.pallas_call(best_kernel, out_shape=(jax.ShapeDtypeStruct((devices, LAN...]
where the time goes in v2:
time: 102 us
  blocking collectives  68.3 us (67%)
  waiting for transfers between devices  10.6 us (10%)
  local copies, waits for them, and re-layouts  9.83 us (10%)
  starting transfers between devices  9.08 us (9%)
  Pallas kernels  3.08 us (3%)
    all_to_all x1, blocking collectives, body(): lax.all_to_all(payload, 'dev', split_axis=0, concat_axis=0, tiled=True)  68.3 us
    all_to_all x1, waiting for transfers between devices, body(): lax.all_to_all(best.reshape(devices, 1, LANES), 'dev', split_axis=0, conc...  10.6 us
    all_to_all x1, starting transfers between devices, body(): lax.all_to_all(best.reshape(devices, 1, LANES), 'dev', split_axis=0, conc...  9.08 us
    all_to_all x2, local copies, waits for them, and re-layouts, body(): lax.all_to_all(payload, 'dev', split_axis=0, concat_axis=0, tiled=True)  5.06 us
    unnamed x14, local copies, waits for them, and re-layouts  4.26 us
  transfers between devices with their start and end apart: 1, of which 1 were waited for; matrix products, arithmetic and copies ran while one was open for 1% of the time, Pallas kernels for 0%

profile of v2, /device:TPU:2, one launch (start us, length us, event | category | flops | bytes accessed | tf_op | source)
XLA Modules:
  0.0 101.7 jit_solution(697993616351058696)
XLA Ops:
  0.6 0.0 copy-start
  0.6 1.6 %copy-done = f32[128,4096]{1,0:T(8,128)S(1)} copy-done((f32[128,4096]{1,0:T(8,128)S(1)}, f32[128,4096]{1,0:T(8,128)}, u32[]{:S(2)}) %copy-start) | copy-done | bytes 2097176
  2.2 0.0 copy-start.1
  2.2 0.7 copy-done.1
  2.9 0.0 copy-start.3
  2.9 0.7 copy-done.3
  3.6 0.0 copy-start.5
  3.6 0.7 copy-done.5
  4.2 0.0 copy-start.6
  4.2 0.7 copy-done.6
  4.9 0.9 place.1
  5.8 2.3 %all_to_all.10 = bf16[128,2,4224]{2,1,0:T(2,128)(2,1)} reshape(bf16[256,4224]{1,0:T(8,128)(2,1)S(1)} %get-tuple-element.9) | data formatting | bytes 4325376 | tf_op jit(solution)/shard_map/all_to_all | solution.py:114
  8.1 68.3 %all_to_all.16 = bf16[128,2,4224]{2,1,0:T(2,128)(2,1)} all-to-all(bf16[128,2,4224]{2,1,0:T(2,128)(2,1)} %all_to_all.10), channel_id=1, replica_groups=mesh['dev'=128,'rep'=2] {'dev'}, dimensions={0} | all-to-all | bytes 4325376 | tf_op jit(solution)/shard_map/all_to_all | solution.py:114
  76.4 0.0 copy-start.2
  76.4 0.0 copy-start.4
  76.4 2.8 %all_to_all.12.got_ref = bf16[256,4224]{1,0:T(8,128)(2,1)S(1)} reshape(bf16[128,2,4224]{2,1,0:T(2,128)(2,1)} %all_to_all.16) | data formatting | bytes 4325376 | tf_op jit(solution)/shard_map/all_to_all | solution.py:114
  79.2 0.0 copy-done.2
  79.2 0.0 copy-done.4
  79.3 1.5 %best.1 = (f32[128,128]{1,0:T(8,128)}, f32[1,128]{1,0:T(1,128)S(1)}) custom-call(bf16[256,4224]{1,0:T(8,128)(2,1)S(1)} %all_to_all.12.got_ref, s32[1,256]{1,0:T(1,128)S(1)} %bitcast.14, s32[1,256]{1,0:T(1,128)S(1)} %bitcast.16), custom_call_target="tpu_custom_call" | custom-call | tf_op jit(solution)/shard_map/best/pallas_call | solution.py:115
  80.8 9.1 %all-to-all-start.1 = ((f32[128,1,128]{2,1,0:T(1,128)}), f32[128,1,128]{2,1,0:T(1,128)S(1)}, u32[]{:S(2)}, u32[]{:S(2)}) async-start(f32[128,1,128]{2,1,0:T(1,128)} %bitcast.5), calls=%async_computation.1 | async-start | bytes 131072 | tf_op jit(solution)/shard_map/all_to_all | solution.py:125
  89.9 0.5 slice_bitcast_fusion
  90.4 10.6 %all-to-all-done.1 = f32[128,1,128]{2,1,0:T(1,128)S(1)} async-done(((f32[128,1,128]{2,1,0:T(1,128)}), f32[128,1,128]{2,1,0:T(1,128)S(1)}, u32[]{:S(2)}, u32[]{:S(2)}) %all-to-all-start.1) | async-done | bytes 65568 | tf_op jit(solution)/shard_map/all_to_all | solution.py:125
  101.0 0.6 pick.1
Async XLA Ops:
  0.6 1.6 %copy-start = (f32[128,4096]{1,0:T(8,128)S(1)}, f32[128,4096]{1,0:T(8,128)}, u32[]{:S(2)}) copy-start(f32[128,4096]{1,0:T(8,128)} %emb_ref.1) | copy-start | bytes 6291460
  2.2 0.7 copy-start.1
  2.9 0.7 copy-start.3
  3.6 0.7 copy-start.5
  4.2 0.7 copy-start.6
  76.4 2.8 %copy-start.2 = (s32[256]{0:T(256)S(1)}, s32[256]{0:T(256)}, u32[]{:S(2)}) copy-start(s32[256]{0:T(256)} %param.8) | copy-start | bytes 3076
  76.4 2.8 %copy-start.4 = (s32[256]{0:T(256)S(1)}, s32[256]{0:T(256)}, u32[]{:S(2)}) copy-start(s32[256]{0:T(256)} %param.9) | copy-start | bytes 3076
  80.8 20.2 %all-to-all-start.1 = ((f32[128,1,128]{2,1,0:T(1,128)}), f32[128,1,128]{2,1,0:T(1,128)S(1)}, u32[]{:S(2)}, u32[]{:S(2)}) async-start(f32[128,1,128]{2,1,0:T(1,128)} %bitcast.5), calls=%async_computation.1 | async-start | bytes 131072 | tf_op jit(solution)/shard_map/all_to_all | solution.py:125

commit v3 on v1

v3 whole, which is shorter than its diff:
```python
import jax
import jax.numpy as jnp
from jax import lax
from jax.experimental import pallas as pl
from jax.experimental.pallas import tpu as pltpu
from jax.sharding import PartitionSpec as P

CAP = 128
LANES = 128
KERNEL_VMEM = 24 * 2**20

norm_eps = 1e-06
cutoff = 0.8


def iota(shape, axis):
    return lax.broadcasted_iota(jnp.int32, shape, axis)


def table_lookup(cluster_row, table_row):
    clusters = table_row.shape[1]
    hit = (iota((clusters, cluster_row.shape[1]), 0) == cluster_row).astype(jnp.bfloat16)
    table = jnp.broadcast_to(table_row.astype(jnp.bfloat16), (8, clusters))
    return jnp.dot(table, hit, preferred_element_type=jnp.float32)[:1]


def place_kernel(emb_ref, table_ref, out_ref, where_ref, own_ref):
    rows, depth = emb_ref.shape
    owners, tiles = out_ref.shape[0], depth // LANES
    clusters = 2 * owners
    ids = table_ref[:, :rows]
    order = table_ref[:, rows : 2 * rows]
    slots = table_ref[:, 2 * rows : 2 * rows + clusters]
    sizes = table_ref[:, 2 * rows + clusters :]
    slot_of = table_lookup(ids, slots).astype(jnp.int32)
    size_of = table_lookup(ids, sizes).astype(jnp.int32)
    where_ref[...] = slot_of
    code = jnp.where(order < size_of, order + 1, 0).astype(jnp.float32)
    hit = iota((clusters, rows), 0) == slot_of
    rank = jnp.sum(jnp.where(hit, code, 0.0), axis=1, keepdims=True)
    coded = jnp.broadcast_to(rank, (clusters, LANES)).astype(jnp.bfloat16)
    out_ref[:, tiles] = coded.reshape(owners, 2, LANES)
    first_slot = lax.axis_index("dev") * 2
    size0 = jnp.sum(jnp.where(slots == first_slot, sizes, 0), axis=1, keepdims=True)
    size1 = jnp.sum(jnp.where(slots == first_slot + 1, sizes, 0), axis=1, keepdims=True)
    own_ref[...] = jnp.where(iota((1, LANES), 1) == 0, size0, size1)
    values = emb_ref[...]
    squares_sum = jnp.sum(values * values, axis=1, keepdims=True)
    unit = (values * lax.rsqrt(squares_sum + norm_eps)).astype(jnp.bfloat16)
    pick = hit.astype(jnp.bfloat16)
    for c in range(0, tiles, 2):
        placed = jnp.dot(
            pick, unit[:, c * LANES : (c + 2) * LANES], preferred_element_type=jnp.float32
        ).astype(jnp.bfloat16)
        out_ref[:, c] = placed[:, :LANES].reshape(owners, 2, LANES)
        out_ref[:, c + 1] = placed[:, LANES:].reshape(owners, 2, LANES)


def best_kernel(got_ref, own_ref, best_ref, mean_ref, matrix, spread_ref):
    sources, tiles = got_ref.shape[:2]
    rows = 2 * sources
    for c in range(tiles):
        matrix[:, c * LANES : (c + 1) * LANES] = got_ref[:, c].reshape(rows, LANES)
    depth = (tiles - 1) * LANES
    unit = matrix[:, :depth]
    coded = matrix[:, depth:]
    similar = lax.dot_general(
        unit, unit, (((1,), (1,)), ((), ())), preferred_element_type=jnp.float32
    )
    rank_col = coded.astype(jnp.float32)[:, :1]
    first = (iota((8, LANES), 1) == 0).astype(jnp.bfloat16)
    rank_row = lax.dot_general(
        first, coded, (((1,), (1,)), ((), ())), preferred_element_type=jnp.float32
    )[:1]
    same = ((iota((rows, rows), 0) ^ iota((rows, rows), 1)) & 1) == 0
    allowed = same & (rank_row > 0.0) & (rank_row < rank_col)
    best = jnp.max(jnp.where(allowed, similar, -1.0), axis=1, keepdims=True)
    spread_ref[...] = jnp.broadcast_to(best, spread_ref.shape)
    live_col = jnp.broadcast_to(rank_col, spread_ref.shape) > 0.0
    summed = jnp.where(live_col, spread_ref[...], 0.0)
    odd = (iota(spread_ref.shape, 0) & 1) == 1
    lane = iota((1, LANES), 1)
    total = jnp.where(
        lane == 0,
        jnp.sum(jnp.where(odd, 0.0, summed), axis=0, keepdims=True),
        jnp.sum(jnp.where(odd, summed, 0.0), axis=0, keepdims=True),
    )
    even_best = spread_ref[pl.ds(0, sources, stride=2), :]
    odd_best = spread_ref[pl.ds(1, sources, stride=2), :]
    best_ref[...] = jnp.where(iota((sources, LANES), 1) == 0, even_best, odd_best)
    mean_ref[...] = total / own_ref[...].astype(jnp.float32)


def pick_kernel(back_ref, where_ref, best_ref, keep_ref):
    slot_of = where_ref[...]
    back = back_ref[...]
    owners = iota((back.shape[0], slot_of.shape[1]), 0)
    from_even = jnp.where(owners * 2 == slot_of, back[:, :1], 0.0)
    from_odd = jnp.where(owners * 2 + 1 == slot_of, back[:, 1:2], 0.0)
    best = jnp.sum(from_even + from_odd, axis=0, keepdims=True)
    best_ref[...] = best
    keep_ref[...] = (best < cutoff).astype(jnp.int32)


def body(embeddings, cluster_id, member_order, cluster_slot, cluster_size):
    devices = lax.axis_size("dev")
    rows, depth = embeddings.shape
    clusters = cluster_slot.shape[0]
    table = jnp.concatenate([cluster_id, member_order, cluster_slot, cluster_size])
    tiles = depth // LANES + 1
    payload, place, own = pl.pallas_call(
        place_kernel,
        out_shape=(
            jax.ShapeDtypeStruct((devices, tiles, 2, LANES), jnp.bfloat16),
            jax.ShapeDtypeStruct((1, rows), jnp.int32),
            jax.ShapeDtypeStruct((1, LANES), jnp.int32),
        ),
        name="place",
        compiler_params=pltpu.CompilerParams(vmem_limit_bytes=KERNEL_VMEM),
    )(embeddings, table.reshape(1, -1))
    got = lax.all_to_all(payload, "dev", split_axis=0, concat_axis=0, tiled=True)
    best, mean = pl.pallas_call(
        best_kernel,
        out_shape=(
            jax.ShapeDtypeStruct((devices, LANES), jnp.float32),
            jax.ShapeDtypeStruct((1, LANES), jnp.float32),
        ),
        scratch_shapes=[
            pltpu.VMEM((clusters, tiles * LANES), jnp.bfloat16),
            pltpu.VMEM((clusters, LANES), jnp.float32),
        ],
        name="best",
        compiler_params=pltpu.CompilerParams(vmem_limit_bytes=KERNEL_VMEM),
    )(got, own)
    back = lax.all_to_all(
        best.reshape(devices, 1, LANES), "dev", split_axis=0, concat_axis=0, tiled=True
    ).reshape(devices, LANES)
    row_best, keep = pl.pallas_call(
        pick_kernel,
        out_shape=(
            jax.ShapeDtypeStruct((1, rows), jnp.float32),
            jax.ShapeDtypeStruct((1, rows), jnp.int32),
        ),
        name="pick",
        compiler_params=pltpu.CompilerParams(vmem_limit_bytes=KERNEL_VMEM),
    )(back, place)
    return (row_best.reshape(rows), keep.reshape(rows), mean[0, :2])


def solution(mesh):
    placed = (P(("rep", "dev"), None), P(("rep", "dev")), P(("rep", "dev")), P("rep"), P("rep"))
    return jax.shard_map(
        body,
        mesh=mesh,
        in_specs=placed,
        out_specs=(P(("rep", "dev")), P(("rep", "dev")), P(("rep", "dev"))),
        check_vma=False,
    )
```

time: 105 us -> 96.3 us (0.917)
  local copies, waits for them, and re-layouts: 8.68 us -> 2.1 us
  Pallas kernels: 8.55 us -> 4.91 us
    all_to_all x2 -> x0, local copies, waits for them, and re-layouts: 6.9 us -> none  [body(): lax.all_to_all(payload, 'dev', split_axis=0, concat_axis=0, tiled=True)]
    pallas_call x1, Pallas kernels: 3.92 us -> 1.89 us  [body(): pl.pallas_call(place_kernel, out_shape=(jax.ShapeDtypeStruct((devices, ti...]
where the time goes in v3:
time: 96.3 us; the launch traced here: 96.1 us
  blocking collectives  68 us (71%)
  waiting for transfers between devices  10.6 us (11%)
  starting transfers between devices  9.02 us (9%)
  Pallas kernels  4.91 us (5%)
  local copies, waits for them, and re-layouts  2.1 us (2%)
    all_to_all x1, blocking collectives, body(): lax.all_to_all(payload, 'dev', split_axis=0, concat_axis=0, tiled=True)  68 us
    all_to_all x1, waiting for transfers between devices, body(): lax.all_to_all(best.reshape(devices, 1, LANES), 'dev', split_axis=0, conc...  10.6 us
    all_to_all x1, starting transfers between devices, body(): lax.all_to_all(best.reshape(devices, 1, LANES), 'dev', split_axis=0, conc...  9.02 us
    pallas_call x1, Pallas kernels, body(): pl.pallas_call(best_kernel, out_shape=(jax.ShapeDtypeStruct((devices, LAN...  2.39 us
  transfers between devices with their start and end apart: 1, of which 1 were waited for; matrix products, arithmetic and copies ran while one was open for 1% of the time, Pallas kernels for 0%

profile of v3, /device:TPU:2, one launch (start us, length us, event | category | flops | bytes accessed | tf_op | source)
XLA Modules:
  0.0 96.1 jit_solution(2541745996831542941)
XLA Ops:
  0.6 0.7 pad_add_fusion
  1.4 0.0 copy-start
  1.4 1.6 %copy-done = f32[128,4096]{1,0:T(8,128)S(1)} copy-done((f32[128,4096]{1,0:T(8,128)S(1)}, f32[128,4096]{1,0:T(8,128)}, u32[]{:S(2)}) %copy-start) | copy-done | bytes 2097176
  2.9 1.9 %place.1 = (bf16[128,33,2,128]{3,2,1,0:T(2,128)(2,1)S(1)}, s32[1,128]{1,0:T(1,128)S(1)}, s32[1,128]{1,0:T(1,128)S(1)}) custom-call(f32[128,4096]{1,0:T(8,128)S(1)} %copy-done, s32[1,768]{1,0:T(1,128)S(1)} %reshape.21.table_ref), custom_call_target="tpu_custom_call" | custom-call | tf_op jit(solution)/shard_map/place/pallas_call | solution.py:111
  4.8 68.0 %all_to_all.10.got_ref = bf16[128,33,2,128]{3,2,1,0:T(2,128)(2,1)S(1)} all-to-all(bf16[128,33,2,128]{3,2,1,0:T(2,128)(2,1)S(1)} %get-tuple-element.10), channel_id=1, replica_groups=mesh['dev'=128,'rep'=2] {'dev'}, dimensions={0} | all-to-all | bytes 4325376 | tf_op jit(solution)/shard_map/all_to_all | solution.py:121
  72.9 2.4 %best.1 = (f32[128,128]{1,0:T(8,128)}, f32[1,128]{1,0:T(1,128)S(1)}) custom-call(bf16[128,33,2,128]{3,2,1,0:T(2,128)(2,1)S(1)} %all_to_all.10.got_ref, s32[1,128]{1,0:T(1,128)S(1)} %get-tuple-element.11.own_ref), custom_call_target="tpu_custom_call" | custom-call | tf_op jit(solution)/shard_map/best/pallas_call | solution.py:122
  75.3 9.0 %all-to-all-start.1 = ((f32[128,1,128]{2,1,0:T(1,128)}), f32[128,1,128]{2,1,0:T(1,128)S(1)}, u32[]{:S(2)}, u32[]{:S(2)}) async-start(f32[128,1,128]{2,1,0:T(1,128)} %bitcast.1), calls=%async_computation.1 | async-start | bytes 131072 | tf_op jit(solution)/shard_map/all_to_all | solution.py:135
  84.3 0.5 slice_bitcast_fusion
  84.8 10.6 %all-to-all-done.1 = f32[128,1,128]{2,1,0:T(1,128)S(1)} async-done(((f32[128,1,128]{2,1,0:T(1,128)}), f32[128,1,128]{2,1,0:T(1,128)S(1)}, u32[]{:S(2)}, u32[]{:S(2)}) %all-to-all-start.1) | async-done | bytes 65568 | tf_op jit(solution)/shard_map/all_to_all | solution.py:135
  95.5 0.6 pick.1
  (1 shorter events, 0.0 us)
Async XLA Ops:
  1.4 1.6 %copy-start = (f32[128,4096]{1,0:T(8,128)S(1)}, f32[128,4096]{1,0:T(8,128)}, u32[]{:S(2)}) copy-start(f32[128,4096]{1,0:T(8,128)} %emb_ref.1) | copy-start | bytes 6291460
  75.3 20.2 %all-to-all-start.1 = ((f32[128,1,128]{2,1,0:T(1,128)}), f32[128,1,128]{2,1,0:T(1,128)S(1)}, u32[]{:S(2)}, u32[]{:S(2)}) async-start(f32[128,1,128]{2,1,0:T(1,128)} %bitcast.1), calls=%async_computation.1 | async-start | bytes 131072 | tf_op jit(solution)/shard_map/all_to_all | solution.py:135

commit v4 on v3

--- a/solution.py
+++ b/solution.py
@@ -8,6 +8,9 @@
 CAP = 128
 LANES = 128
 KERNEL_VMEM = 24 * 2**20
+STEP = 8
+IN_PARTS = 8
+UNIT_VMEM = 52 * 2**20
 
 norm_eps = 1e-06
 cutoff = 0.8
@@ -24,14 +27,34 @@
     return jnp.dot(table, hit, preferred_element_type=jnp.float32)[:1]
 
 
-def place_kernel(emb_ref, table_ref, out_ref, where_ref, own_ref):
-    rows, depth = emb_ref.shape
+def unit_kernel(emb_ref, unit_ref, emb, sems):
+    rows = emb.shape[0]
+    part = rows // IN_PARTS
+    copies = [
+        pltpu.make_async_copy(
+            emb_ref.at[pl.ds(k * part, part)], emb.at[pl.ds(k * part, part)], sems.at[k]
+        )
+        for k in range(IN_PARTS)
+    ]
+    for copy in copies:
+        copy.start()
+    for k, copy in enumerate(copies):
+        copy.wait()
+        values = emb[k * part : (k + 1) * part]
+        squares_sum = jnp.sum(values * values, axis=1, keepdims=True)
+        unit_ref[k * part : (k + 1) * part] = (
+            values * lax.rsqrt(squares_sum + norm_eps)
+        ).astype(jnp.bfloat16)
+
+
+def place_kernel(unit_ref, id_ref, order_ref, slot_ref, size_ref, out_ref, where_ref, own_ref):
+    rows, depth = unit_ref.shape
     owners, tiles = out_ref.shape[0], depth // LANES
     clusters = 2 * owners
-    ids = table_ref[:, :rows]
-    order = table_ref[:, rows : 2 * rows]
-    slots = table_ref[:, 2 * rows : 2 * rows + clusters]
-    sizes = table_ref[:, 2 * rows + clusters :]
+    ids = id_ref[...]
+    slots = slot_ref[...]
+    sizes = size_ref[...]
+    order = order_ref[...]
     slot_of = table_lookup(ids, slots).astype(jnp.int32)
     size_of = table_lookup(ids, sizes).astype(jnp.int32)
     where_ref[...] = slot_of
@@ -44,29 +67,27 @@
     size0 = jnp.sum(jnp.where(slots == first_slot, sizes, 0), axis=1, keepdims=True)
     size1 = jnp.sum(jnp.where(slots == first_slot + 1, sizes, 0), axis=1, keepdims=True)
     own_ref[...] = jnp.where(iota((1, LANES), 1) == 0, size0, size1)
-    values = emb_ref[...]
-    squares_sum = jnp.sum(values * values, axis=1, keepdims=True)
-    unit = (values * lax.rsqrt(squares_sum + norm_eps)).astype(jnp.bfloat16)
     pick = hit.astype(jnp.bfloat16)
     for c in range(0, tiles, 2):
         placed = jnp.dot(
-            pick, unit[:, c * LANES : (c + 2) * LANES], preferred_element_type=jnp.float32
+            pick, unit_ref[:, c * LANES : (c + 2) * LANES], preferred_element_type=jnp.float32
         ).astype(jnp.bfloat16)
         out_ref[:, c] = placed[:, :LANES].reshape(owners, 2, LANES)
         out_ref[:, c + 1] = placed[:, LANES:].reshape(owners, 2, LANES)
 
 
-def best_kernel(got_ref, own_ref, best_ref, mean_ref, matrix, spread_ref):
-    sources, tiles = got_ref.shape[:2]
+def best_kernel(got_ref, own_ref, best_ref, mean_ref, spread_ref):
+    sources, tiles = got_ref.shape[0], got_ref.shape[1] - 1
     rows = 2 * sources
-    for c in range(tiles):
-        matrix[:, c * LANES : (c + 1) * LANES] = got_ref[:, c].reshape(rows, LANES)
-    depth = (tiles - 1) * LANES
-    unit = matrix[:, :depth]
-    coded = matrix[:, depth:]
-    similar = lax.dot_general(
-        unit, unit, (((1,), (1,)), ((), ())), preferred_element_type=jnp.float32
-    )
+    similar = jnp.zeros((rows, rows), jnp.float32)
+    for q in range(0, tiles, STEP):
+        unit = jnp.concatenate(
+            [got_ref[:, c].reshape(rows, LANES) for c in range(q, q + STEP)], axis=1
+        )
+        similar += lax.dot_general(
+            unit, unit, (((1,), (1,)), ((), ())), preferred_element_type=jnp.float32
+        )
+    coded = got_ref[:, tiles].reshape(rows, LANES)
     rank_col = coded.astype(jnp.float32)[:, :1]
     first = (iota((8, LANES), 1) == 0).astype(jnp.bfloat16)
     rank_row = lax.dot_general(
@@ -106,8 +127,18 @@
     devices = lax.axis_size("dev")
     rows, depth = embeddings.shape
     clusters = cluster_slot.shape[0]
-    table = jnp.concatenate([cluster_id, member_order, cluster_slot, cluster_size])
     tiles = depth // LANES + 1
+    unit = pl.pallas_call(
+        unit_kernel,
+        out_shape=jax.ShapeDtypeStruct((rows, depth), jnp.bfloat16),
+        in_specs=[pl.BlockSpec(memory_space=pltpu.HBM)],
+        scratch_shapes=[
+            pltpu.VMEM((rows, depth), jnp.float32),
+            pltpu.SemaphoreType.DMA((IN_PARTS,)),
+        ],
+        name="unit",
+        compiler_params=pltpu.CompilerParams(vmem_limit_bytes=UNIT_VMEM),
+    )(embeddings)
     payload, place, own = pl.pallas_call(
         place_kernel,
         out_shape=(
@@ -117,7 +148,13 @@
         ),
         name="place",
         compiler_params=pltpu.CompilerParams(vmem_limit_bytes=KERNEL_VMEM),
-    )(embeddings, table.reshape(1, -1))
+    )(
+        unit,
+        cluster_id.reshape(1, rows),
+        member_order.reshape(1, rows),
+        cluster_slot.reshape(1, clusters),
+        cluster_size.reshape(1, clusters),
+    )
     got = lax.all_to_all(payload, "dev", split_axis=0, concat_axis=0, tiled=True)
     best, mean = pl.pallas_call(
         best_kernel,
@@ -126,7 +163,6 @@
             jax.ShapeDtypeStruct((1, LANES), jnp.float32),
         ),
         scratch_shapes=[
-            pltpu.VMEM((clusters, tiles * LANES), jnp.bfloat16),
             pltpu.VMEM((clusters, LANES), jnp.float32),
         ],
         name="best",

time: 96.3 us -> 95.9 us (level)
  Pallas kernels: 4.91 us -> 6.65 us
  local copies, waits for them, and re-layouts: 2.1 us -> 0.53 us
    pallas_call x0 -> x1, Pallas kernels: none -> 2.13 us  [body(): pl.pallas_call(unit_kernel, out_shape=jax.ShapeDtypeStruct((rows, depth),...]
    unnamed x2 -> x8, local copies, waits for them, and re-layouts: 1.59 us -> 0.02 us
where the time goes in v4:
time: 95.9 us; the launch traced here: 95.7 us
  blocking collectives  68 us (71%)
  waiting for transfers between devices  10.6 us (11%)
  starting transfers between devices  9.08 us (9%)
  Pallas kernels  6.65 us (7%)
    all_to_all x1, blocking collectives, body(): lax.all_to_all(payload, 'dev', split_axis=0, concat_axis=0, tiled=True)  68 us
    all_to_all x1, waiting for transfers between devices, body(): lax.all_to_all(best.reshape(devices, 1, LANES), 'dev', split_axis=0, conc...  10.6 us
    all_to_all x1, starting transfers between devices, body(): lax.all_to_all(best.reshape(devices, 1, LANES), 'dev', split_axis=0, conc...  9.08 us
    pallas_call x1, Pallas kernels, body(): pl.pallas_call(best_kernel, out_shape=(jax.ShapeDtypeStruct((devices, LAN...  2.13 us
    pallas_call x1, Pallas kernels, body(): pl.pallas_call(unit_kernel, out_shape=jax.ShapeDtypeStruct((rows, depth),...  2.13 us
  transfers between devices with their start and end apart: 1, of which 1 were waited for; matrix products, arithmetic and copies ran while one was open for 1% of the time, Pallas kernels for 0%

profile of v4, /device:TPU:2, one launch (start us, length us, event | category | flops | bytes accessed | tf_op | source)
XLA Modules:
  0.0 95.7 jit_solution(11414480147956843763)
XLA Ops:
  0.6 0.0 copy-start.1
  0.6 0.0 copy-start
  0.7 0.0 copy-start.3
  0.7 0.0 copy-start.2
  0.7 2.1 %unit.1.unit_ref = bf16[128,4096]{1,0:T(8,128)(2,1)S(1)} custom-call(f32[128,4096]{1,0:T(8,128)} %emb_ref.1), custom_call_target="tpu_custom_call" | custom-call | tf_op jit(solution)/shard_map/unit/pallas_call | solution.py:131
  2.8 0.0 copy-done.1
  2.8 0.0 copy-done
  2.8 0.0 copy-done.3
  2.8 0.0 copy-done.2
  2.9 1.8 %place.1 = (bf16[128,33,2,128]{3,2,1,0:T(2,128)(2,1)S(1)}, s32[1,128]{1,0:T(1,128)S(1)}, s32[1,128]{1,0:T(1,128)S(1)}) custom-call(bf16[128,4096]{1,0:T(8,128)(2,1)S(1)} %unit.1.unit_ref, s32[1,128]{1,0:T(1,128)S(1)} %bitcast.15, s32[1,128]{1,0:T(1,128)S(1)} %bitcast.16, s32[1,256]{1,0:T(1,128)S(1)} %bitcast.13, s32[1,256]{1,0:T(1,128)S(1)} %bitcast.14), custom_call_target="tpu_custom_call" | custom-call | tf_op jit(solution)/shard_map/place/pallas_call | solution.py:142
  4.6 68.0 %all_to_all.10.got_ref = bf16[128,33,2,128]{3,2,1,0:T(2,128)(2,1)S(1)} all-to-all(bf16[128,33,2,128]{3,2,1,0:T(2,128)(2,1)S(1)} %get-tuple-element.10), channel_id=1, replica_groups=mesh['dev'=128,'rep'=2] {'dev'}, dimensions={0} | all-to-all | bytes 4325376 | tf_op jit(solution)/shard_map/all_to_all | solution.py:158
  72.7 2.1 %best.1 = (f32[128,128]{1,0:T(8,128)}, f32[1,128]{1,0:T(1,128)S(1)}) custom-call(bf16[128,33,2,128]{3,2,1,0:T(2,128)(2,1)S(1)} %all_to_all.10.got_ref, s32[1,128]{1,0:T(1,128)S(1)} %get-tuple-element.11.own_ref), custom_call_target="tpu_custom_call" | custom-call | tf_op jit(solution)/shard_map/best/pallas_call | solution.py:159
  74.8 9.1 %all-to-all-start.1 = ((f32[128,1,128]{2,1,0:T(1,128)}), f32[128,1,128]{2,1,0:T(1,128)S(1)}, u32[]{:S(2)}, u32[]{:S(2)}) async-start(f32[128,1,128]{2,1,0:T(1,128)} %bitcast.5), calls=%async_computation.1 | async-start | bytes 131072 | tf_op jit(solution)/shard_map/all_to_all | solution.py:171
  83.9 0.5 slice_bitcast_fusion
  84.4 10.6 %all-to-all-done.1 = f32[128,1,128]{2,1,0:T(1,128)S(1)} async-done(((f32[128,1,128]{2,1,0:T(1,128)}), f32[128,1,128]{2,1,0:T(1,128)S(1)}, u32[]{:S(2)}, u32[]{:S(2)}) %all-to-all-start.1) | async-done | bytes 65568 | tf_op jit(solution)/shard_map/all_to_all | solution.py:171
  95.0 0.6 pick.1
Async XLA Ops:
  0.6 2.2 %copy-start.1 = (s32[256]{0:T(256)S(1)}, s32[256]{0:T(256)}, u32[]{:S(2)}) copy-start(s32[256]{0:T(256)} %param.9) | copy-start | bytes 3076
  0.6 2.2 %copy-start = (s32[256]{0:T(256)S(1)}, s32[256]{0:T(256)}, u32[]{:S(2)}) copy-start(s32[256]{0:T(256)} %param.8) | copy-start | bytes 3076
  0.7 2.2 %copy-start.3 = (s32[128]{0:T(128)S(1)}, s32[128]{0:T(128)}, u32[]{:S(2)}) copy-start(s32[128]{0:T(128)} %param.7) | copy-start | bytes 1540
  0.7 2.2 %copy-start.2 = (s32[128]{0:T(128)S(1)}, s32[128]{0:T(128)}, u32[]{:S(2)}) copy-start(s32[128]{0:T(128)} %param.6) | copy-start | bytes 1540
  74.8 20.2 %all-to-all-start.1 = ((f32[128,1,128]{2,1,0:T(1,128)}), f32[128,1,128]{2,1,0:T(1,128)S(1)}, u32[]{:S(2)}, u32[]{:S(2)}) async-start(f32[128,1,128]{2,1,0:T(1,128)} %bitcast.5), calls=%async_computation.1 | async-start | bytes 131072 | tf_op jit(solution)/shard_map/all_to_all | solution.py:171

commit v5 on v4

--- a/solution.py
+++ b/solution.py
@@ -109,7 +109,7 @@
     even_best = spread_ref[pl.ds(0, sources, stride=2), :]
     odd_best = spread_ref[pl.ds(1, sources, stride=2), :]
     best_ref[...] = jnp.where(iota((sources, LANES), 1) == 0, even_best, odd_best)
-    mean_ref[...] = total / own_ref[...].astype(jnp.float32)
+    mean_ref[...] = (total / own_ref[...].astype(jnp.float32))[:, : mean_ref.shape[1]]
 
 
 def pick_kernel(back_ref, where_ref, best_ref, keep_ref):
@@ -160,7 +160,7 @@
         best_kernel,
         out_shape=(
             jax.ShapeDtypeStruct((devices, LANES), jnp.float32),
-            jax.ShapeDtypeStruct((1, LANES), jnp.float32),
+            jax.ShapeDtypeStruct((1, 2), jnp.float32),
         ),
         scratch_shapes=[
             pltpu.VMEM((clusters, LANES), jnp.float32),
@@ -180,7 +180,7 @@
         name="pick",
         compiler_params=pltpu.CompilerParams(vmem_limit_bytes=KERNEL_VMEM),
     )(back, place)
-    return (row_best.reshape(rows), keep.reshape(rows), mean[0, :2])
+    return (row_best.reshape(rows), keep.reshape(rows), mean.reshape(2))
 
 
 def solution(mesh):

time: 95.9 us -> 95.1 us (level)
  blocking collectives: 68 us -> 87.6 us
  waiting for transfers between devices: 10.6 us -> 0 us
  starting transfers between devices: 9.08 us -> 0 us
    all_to_all x0 -> x1, blocking collectives: none -> 19.6 us  [body(): lax.all_to_all(best.reshape(devices, 1, LANES), 'dev', split_axis=0, conc...]
    all_to_all x1 -> x0, waiting for transfers between devices: 10.6 us -> none  [body(): lax.all_to_all(best.reshape(devices, 1, LANES), 'dev', split_axis=0, conc...]
    all_to_all x1 -> x0, starting transfers between devices: 9.08 us -> none  [body(): lax.all_to_all(best.reshape(devices, 1, LANES), 'dev', split_axis=0, conc...]
  transfers between devices with their start and end apart: 1 -> 0, of which waited for: 1 -> 0; matrix products, arithmetic and copies ran while one was open for 1% -> 0% of each run, Pallas kernels for 0% -> 0%
where the time goes in v5:
time: 95.1 us; the launch traced here: 94.9 us
  blocking collectives  87.6 us (92%)
  Pallas kernels  6.57 us (7%)
    all_to_all x1, blocking collectives, body(): lax.all_to_all(payload, 'dev', split_axis=0, concat_axis=0, tiled=True)  68 us
    all_to_all x1, blocking collectives, body(): lax.all_to_all(best.reshape(devices, 1, LANES), 'dev', split_axis=0, conc...  19.6 us
    pallas_call x1, Pallas kernels, body(): pl.pallas_call(unit_kernel, out_shape=jax.ShapeDtypeStruct((rows, depth),...  2.13 us
    pallas_call x1, Pallas kernels, body(): pl.pallas_call(best_kernel, out_shape=(jax.ShapeDtypeStruct((devices, LAN...  2.05 us

profile of v5, /device:TPU:2, one launch (start us, length us, event | category | flops | bytes accessed | tf_op | source)
XLA Modules:
  0.0 94.9 jit_solution(4525600003645181323)
XLA Ops:
  0.6 0.0 copy-start.1
  0.6 0.0 copy-start
  0.7 0.0 copy-start.3
  0.7 0.0 copy-start.2
  0.7 2.1 %unit.1.unit_ref = bf16[128,4096]{1,0:T(8,128)(2,1)S(1)} custom-call(f32[128,4096]{1,0:T(8,128)} %emb_ref.1), custom_call_target="tpu_custom_call" | custom-call | tf_op jit(solution)/shard_map/unit/pallas_call | solution.py:131
  2.8 0.0 copy-done.1
  2.8 0.0 copy-done
  2.8 0.0 copy-done.3
  2.8 0.0 copy-done.2
  2.9 1.8 %place.1 = (bf16[128,33,2,128]{3,2,1,0:T(2,128)(2,1)S(1)}, s32[1,128]{1,0:T(1,128)S(1)}, s32[1,128]{1,0:T(1,128)S(1)}) custom-call(bf16[128,4096]{1,0:T(8,128)(2,1)S(1)} %unit.1.unit_ref, s32[1,128]{1,0:T(1,128)S(1)} %bitcast.15, s32[1,128]{1,0:T(1,128)S(1)} %bitcast.16, s32[1,256]{1,0:T(1,128)S(1)} %bitcast.13, s32[1,256]{1,0:T(1,128)S(1)} %bitcast.14), custom_call_target="tpu_custom_call" | custom-call | tf_op jit(solution)/shard_map/place/pallas_call | solution.py:142
  4.6 68.0 %all_to_all.10.got_ref = bf16[128,33,2,128]{3,2,1,0:T(2,128)(2,1)S(1)} all-to-all(bf16[128,33,2,128]{3,2,1,0:T(2,128)(2,1)S(1)} %get-tuple-element.10), channel_id=1, replica_groups=mesh['dev'=128,'rep'=2] {'dev'}, dimensions={0} | all-to-all | bytes 4325376 | tf_op jit(solution)/shard_map/all_to_all | solution.py:158
  72.7 2.0 %best.1 = (f32[128,128]{1,0:T(8,128)S(1)}, f32[1,2]{1,0:T(1,128)}) custom-call(bf16[128,33,2,128]{3,2,1,0:T(2,128)(2,1)S(1)} %all_to_all.10.got_ref, s32[1,128]{1,0:T(1,128)S(1)} %get-tuple-element.11.own_ref), custom_call_target="tpu_custom_call" | custom-call | tf_op jit(solution)/shard_map/best/pallas_call | solution.py:159
  74.7 19.6 %all_to_all.11 = f32[128,1,128]{2,1,0:T(1,128)S(1)} all-to-all(f32[128,1,128]{2,1,0:T(1,128)S(1)} %bitcast.12), channel_id=1, replica_groups=mesh['dev'=128,'rep'=2] {'dev'}, dimensions={0} | all-to-all | bytes 131072 | tf_op jit(solution)/shard_map/all_to_all | solution.py:171
  94.3 0.6 pick.1
Async XLA Ops:
  0.6 2.2 %copy-start.1 = (s32[256]{0:T(256)S(1)}, s32[256]{0:T(256)}, u32[]{:S(2)}) copy-start(s32[256]{0:T(256)} %param.9) | copy-start | bytes 3076
  0.6 2.2 %copy-start = (s32[256]{0:T(256)S(1)}, s32[256]{0:T(256)}, u32[]{:S(2)}) copy-start(s32[256]{0:T(256)} %param.8) | copy-start | bytes 3076
  0.7 2.2 %copy-start.3 = (s32[128]{0:T(128)S(1)}, s32[128]{0:T(128)}, u32[]{:S(2)}) copy-start(s32[128]{0:T(128)} %param.7) | copy-start | bytes 1540
  0.7 2.2 %copy-start.2 = (s32[128]{0:T(128)S(1)}, s32[128]{0:T(128)}, u32[]{:S(2)}) copy-start(s32[128]{0:T(128)} %param.6) | copy-start | bytes 1540

commit v6 on v5

--- a/solution.py
+++ b/solution.py
@@ -10,7 +10,6 @@
 KERNEL_VMEM = 24 * 2**20
 STEP = 8
 IN_PARTS = 8
-UNIT_VMEM = 52 * 2**20
 
 norm_eps = 1e-06
 cutoff = 0.8
@@ -27,34 +26,35 @@
     return jnp.dot(table, hit, preferred_element_type=jnp.float32)[:1]
 
 
-def unit_kernel(emb_ref, unit_ref, emb, sems):
-    rows = emb.shape[0]
+def place_kernel(
+    emb_ref, id_ref, order_ref, slot_ref, size_ref,
+    out_ref, where_ref, own_ref,
+    emb, unit, ids_v, order_v, slot_v, size_v, sems,
+):
+    rows, depth = emb.shape
     part = rows // IN_PARTS
-    copies = [
+    owners, tiles = out_ref.shape[0], depth // LANES
+    clusters = 2 * owners
+    small = [
+        pltpu.make_async_copy(source, target, sems.at[k])
+        for k, (source, target) in enumerate(
+            ((id_ref, ids_v), (slot_ref, slot_v), (order_ref, order_v), (size_ref, size_v))
+        )
+    ]
+    large = [
         pltpu.make_async_copy(
-            emb_ref.at[pl.ds(k * part, part)], emb.at[pl.ds(k * part, part)], sems.at[k]
+            emb_ref.at[pl.ds(k * part, part)], emb.at[pl.ds(k * part, part)], sems.at[4 + k]
         )
         for k in range(IN_PARTS)
     ]
-    for copy in copies:
+    for copy in small + large:
         copy.start()
-    for k, copy in enumerate(copies):
+    for copy in small:
         copy.wait()
-        values = emb[k * part : (k + 1) * part]
-        squares_sum = jnp.sum(values * values, axis=1, keepdims=True)
-        unit_ref[k * part : (k + 1) * part] = (
-            values * lax.rsqrt(squares_sum + norm_eps)
-        ).astype(jnp.bfloat16)
-
-
-def place_kernel(unit_ref, id_ref, order_ref, slot_ref, size_ref, out_ref, where_ref, own_ref):
-    rows, depth = unit_ref.shape
-    owners, tiles = out_ref.shape[0], depth // LANES
-    clusters = 2 * owners
-    ids = id_ref[...]
-    slots = slot_ref[...]
-    sizes = size_ref[...]
-    order = order_ref[...]
+    ids = ids_v[...]
+    order = order_v[...]
+    slots = slot_v[...]
+    sizes = size_v[...]
     slot_of = table_lookup(ids, slots).astype(jnp.int32)
     size_of = table_lookup(ids, sizes).astype(jnp.int32)
     where_ref[...] = slot_of
@@ -68,9 +68,16 @@
     size1 = jnp.sum(jnp.where(slots == first_slot + 1, sizes, 0), axis=1, keepdims=True)
     own_ref[...] = jnp.where(iota((1, LANES), 1) == 0, size0, size1)
     pick = hit.astype(jnp.bfloat16)
+    for k, copy in enumerate(large):
+        copy.wait()
+        values = emb[k * part : (k + 1) * part]
+        squares_sum = jnp.sum(values * values, axis=1, keepdims=True)
+        unit[k * part : (k + 1) * part] = (
+            values * lax.rsqrt(squares_sum + norm_eps)
+        ).astype(jnp.bfloat16)
     for c in range(0, tiles, 2):
         placed = jnp.dot(
-            pick, unit_ref[:, c * LANES : (c + 2) * LANES], preferred_element_type=jnp.float32
+            pick, unit[:, c * LANES : (c + 2) * LANES], preferred_element_type=jnp.float32
         ).astype(jnp.bfloat16)
         out_ref[:, c] = placed[:, :LANES].reshape(owners, 2, LANES)
         out_ref[:, c + 1] = placed[:, LANES:].reshape(owners, 2, LANES)
@@ -128,17 +135,13 @@
     rows, depth = embeddings.shape
     clusters = cluster_slot.shape[0]
     tiles = depth // LANES + 1
-    unit = pl.pallas_call(
-        unit_kernel,
-        out_shape=jax.ShapeDtypeStruct((rows, depth), jnp.bfloat16),
-        in_specs=[pl.BlockSpec(memory_space=pltpu.HBM)],
-        scratch_shapes=[
-            pltpu.VMEM((rows, depth), jnp.float32),
-            pltpu.SemaphoreType.DMA((IN_PARTS,)),
-        ],
-        name="unit",
-        compiler_params=pltpu.CompilerParams(vmem_limit_bytes=UNIT_VMEM),
-    )(embeddings)
+    sources = (
+        embeddings,
+        cluster_id.reshape(1, rows),
+        member_order.reshape(1, rows),
+        cluster_slot.reshape(1, clusters),
+        cluster_size.reshape(1, clusters),
+    )
     payload, place, own = pl.pallas_call(
         place_kernel,
         out_shape=(
@@ -146,15 +149,19 @@
             jax.ShapeDtypeStruct((1, rows), jnp.int32),
             jax.ShapeDtypeStruct((1, LANES), jnp.int32),
         ),
+        in_specs=[pl.BlockSpec(memory_space=pltpu.HBM)] * len(sources),
+        scratch_shapes=[
+            pltpu.VMEM((rows, depth), jnp.float32),
+            pltpu.VMEM((rows, depth), jnp.bfloat16),
+            pltpu.VMEM((1, rows), jnp.int32),
+            pltpu.VMEM((1, rows), jnp.int32),
+            pltpu.VMEM((1, clusters), jnp.int32),
+            pltpu.VMEM((1, clusters), jnp.int32),
+            pltpu.SemaphoreType.DMA((4 + IN_PARTS,)),
+        ],
         name="place",
         compiler_params=pltpu.CompilerParams(vmem_limit_bytes=KERNEL_VMEM),
-    )(
-        unit,
-        cluster_id.reshape(1, rows),
-        member_order.reshape(1, rows),
-        cluster_slot.reshape(1, clusters),
-        cluster_size.reshape(1, clusters),
-    )
+    )(*[pltpu.with_memory_space_constraint(x, pltpu.HBM) for x in sources])
     got = lax.all_to_all(payload, "dev", split_axis=0, concat_axis=0, tiled=True)
     best, mean = pl.pallas_call(
         best_kernel,

time: 95.1 us -> 94.9 us (level)
    pallas_call x1 -> x0, Pallas kernels: 2.13 us -> none  [body(): pl.pallas_call(unit_kernel, out_shape=jax.ShapeDtypeStruct((rows, depth),...]
    pallas_call x1, Pallas kernels: 1.76 us -> 3.76 us  [body(): pl.pallas_call(place_kernel, out_shape=(jax.ShapeDtypeStruct((devices, ti...]
where the time goes in v6:
time: 94.9 us; the launch traced here: 94.7 us
  blocking collectives  87.6 us (92%)
  Pallas kernels  6.44 us (7%)
    all_to_all x1, blocking collectives, body(): lax.all_to_all(payload, 'dev', split_axis=0, concat_axis=0, tiled=True)  68 us
    all_to_all x1, blocking collectives, body(): lax.all_to_all(best.reshape(devices, 1, LANES), 'dev', split_axis=0, conc...  19.6 us
    pallas_call x1, Pallas kernels, body(): pl.pallas_call(place_kernel, out_shape=(jax.ShapeDtypeStruct((devices, ti...  3.76 us
    pallas_call x1, Pallas kernels, body(): pl.pallas_call(best_kernel, out_shape=(jax.ShapeDtypeStruct((devices, LAN...  2.05 us

profile of v6, /device:TPU:2, one launch (start us, length us, event | category | flops | bytes accessed | tf_op | source)
XLA Modules:
  0.0 94.7 jit_solution(704286854674703042)
XLA Ops:
  0.6 3.8 %place.1 = (bf16[128,33,2,128]{3,2,1,0:T(2,128)(2,1)S(1)}, s32[1,128]{1,0:T(1,128)S(1)}, s32[1,128]{1,0:T(1,128)S(1)}) custom-call(f32[128,4096]{1,0:T(8,128)} %emb_ref.1, s32[1,128]{1,0:T(1,128)} %bitcast.15, s32[1,128]{1,0:T(1,128)} %bitcast.16, s32[1,256]{1,0:T(1,128)} %bitcast.13, s32[1,256]{1,0:T(1,128)} %bitcast.14), custom_call_target="tpu_custom_call" | custom-call | tf_op jit(solution)/shard_map/place/pallas_call | solution.py:145
  4.4 68.0 %all_to_all.10.got_ref = bf16[128,33,2,128]{3,2,1,0:T(2,128)(2,1)S(1)} all-to-all(bf16[128,33,2,128]{3,2,1,0:T(2,128)(2,1)S(1)} %get-tuple-element.10), channel_id=1, replica_groups=mesh['dev'=128,'rep'=2] {'dev'}, dimensions={0} | all-to-all | bytes 4325376 | tf_op jit(solution)/shard_map/all_to_all | solution.py:165
  72.4 2.0 %best.1 = (f32[128,128]{1,0:T(8,128)S(1)}, f32[1,2]{1,0:T(1,128)}) custom-call(bf16[128,33,2,128]{3,2,1,0:T(2,128)(2,1)S(1)} %all_to_all.10.got_ref, s32[1,128]{1,0:T(1,128)S(1)} %get-tuple-element.11.own_ref), custom_call_target="tpu_custom_call" | custom-call | tf_op jit(solution)/shard_map/best/pallas_call | solution.py:166
  74.5 19.6 %all_to_all.11 = f32[128,1,128]{2,1,0:T(1,128)S(1)} all-to-all(f32[128,1,128]{2,1,0:T(1,128)S(1)} %bitcast.12), channel_id=1, replica_groups=mesh['dev'=128,'rep'=2] {'dev'}, dimensions={0} | all-to-all | bytes 131072 | tf_op jit(solution)/shard_map/all_to_all | solution.py:178
  94.1 0.6 pick.1

commit v7 on v6

--- a/solution.py
+++ b/solution.py
@@ -24,6 +24,21 @@
     hit = (iota((clusters, cluster_row.shape[1]), 0) == cluster_row).astype(jnp.bfloat16)
     table = jnp.broadcast_to(table_row.astype(jnp.bfloat16), (8, clusters))
     return jnp.dot(table, hit, preferred_element_type=jnp.float32)[:1]
+
+
+def chunk_of(device, devices):
+    return devices - 1 - device
+
+
+def chunk_slot(slot, devices):
+    return chunk_of(slot >> 1, devices) * 2 + (slot & 1)
+
+
+def exchange(x, devices):
+    order = sorted(range(devices), key=lambda device: chunk_of(device, devices))
+    return lax.all_to_all(
+        x, "dev", split_axis=0, concat_axis=0, axis_index_groups=[order], tiled=True
+    )
 
 
 def place_kernel(
@@ -55,7 +70,7 @@
     order = order_v[...]
     slots = slot_v[...]
     sizes = size_v[...]
-    slot_of = table_lookup(ids, slots).astype(jnp.int32)
+    slot_of = chunk_slot(table_lookup(ids, slots).astype(jnp.int32), owners)
     size_of = table_lookup(ids, sizes).astype(jnp.int32)
     where_ref[...] = slot_of
     code = jnp.where(order < size_of, order + 1, 0).astype(jnp.float32)
@@ -162,7 +177,7 @@
         name="place",
         compiler_params=pltpu.CompilerParams(vmem_limit_bytes=KERNEL_VMEM),
     )(*[pltpu.with_memory_space_constraint(x, pltpu.HBM) for x in sources])
-    got = lax.all_to_all(payload, "dev", split_axis=0, concat_axis=0, tiled=True)
+    got = exchange(payload, devices)
     best, mean = pl.pallas_call(
         best_kernel,
         out_shape=(
@@ -175,9 +190,7 @@
         name="best",
         compiler_params=pltpu.CompilerParams(vmem_limit_bytes=KERNEL_VMEM),
     )(got, own)
-    back = lax.all_to_all(
-        best.reshape(devices, 1, LANES), "dev", split_axis=0, concat_axis=0, tiled=True
-    ).reshape(devices, LANES)
+    back = exchange(best.reshape(devices, 1, LANES), devices).reshape(devices, LANES)
     row_best, keep = pl.pallas_call(
         pick_kernel,
         out_shape=(

time: 94.9 us -> 91.1 us (0.960)
  blocking collectives: 87.6 us -> 83.3 us
    all_to_all x2, blocking collectives: 87.6 us -> 83.3 us  [exchange(): lax.all_to_all(x, 'dev', split_axis=0, concat_axis=0, axis_index_groups=[...]
where the time goes in v7:
time: 91.1 us; the launch traced here: 90.4 us
  blocking collectives  83.3 us (91%)
  Pallas kernels  6.43 us (7%)
    all_to_all x2, blocking collectives, exchange(): lax.all_to_all(x, 'dev', split_axis=0, concat_axis=0, axis_index_groups=[...  83.3 us
    pallas_call x1, Pallas kernels, body(): pl.pallas_call(place_kernel, out_shape=(jax.ShapeDtypeStruct((devices, ti...  3.76 us
    pallas_call x1, Pallas kernels, body(): pl.pallas_call(best_kernel, out_shape=(jax.ShapeDtypeStruct((devices, LAN...  2.05 us

profile of v7, /device:TPU:2, one launch (start us, length us, event | category | flops | bytes accessed | tf_op | source)
XLA Modules:
  0.0 90.4 jit_solution(2300424693917301927)
XLA Ops:
  0.6 3.8 %place.1 = (bf16[128,33,2,128]{3,2,1,0:T(2,128)(2,1)S(1)}, s32[1,128]{1,0:T(1,128)S(1)}, s32[1,128]{1,0:T(1,128)S(1)}) custom-call(f32[128,4096]{1,0:T(8,128)} %emb_ref.1, s32[1,128]{1,0:T(1,128)} %bitcast.15, s32[1,128]{1,0:T(1,128)} %bitcast.16, s32[1,256]{1,0:T(1,128)} %bitcast.13, s32[1,256]{1,0:T(1,128)} %bitcast.14), custom_call_target="tpu_custom_call" | custom-call | tf_op jit(solution)/shard_map/place/pallas_call | solution.py:160
  4.4 64.6 %all_to_all.10.got_ref = bf16[128,33,2,128]{3,2,1,0:T(2,128)(2,1)S(1)} all-to-all(bf16[128,33,2,128]{3,2,1,0:T(2,128)(2,1)S(1)} %get-tuple-element.10), channel_id=1, replica_groups={{254,252,250,248,246,244,242,240,238,236,234,232,230,228,226,224,222,22..., dimensions={0} | all-to-all | bytes 4325376 | tf_op jit(solution)/shard_map/all_to_all | solution.py:39
  69.0 2.0 %best.1 = (f32[128,128]{1,0:T(8,128)S(1)}, f32[1,2]{1,0:T(1,128)}) custom-call(bf16[128,33,2,128]{3,2,1,0:T(2,128)(2,1)S(1)} %all_to_all.10.got_ref, s32[1,128]{1,0:T(1,128)S(1)} %get-tuple-element.11.own_ref), custom_call_target="tpu_custom_call" | custom-call | tf_op jit(solution)/shard_map/best/pallas_call | solution.py:181
  71.0 18.7 %all_to_all.11 = f32[128,1,128]{2,1,0:T(1,128)S(1)} all-to-all(f32[128,1,128]{2,1,0:T(1,128)S(1)} %bitcast.12), channel_id=1, replica_groups={{254,252,250,248,246,244,242,240,238,236,234,232,230,228,226,224,222,22..., dimensions={0} | all-to-all | bytes 131072 | tf_op jit(solution)/shard_map/all_to_all | solution.py:39
  89.7 0.6 pick.1

commit v8 on v7

--- a/solution.py
+++ b/solution.py
@@ -27,7 +27,8 @@
 
 
 def chunk_of(device, devices):
-    return devices - 1 - device
+    y, x, z = device >> 5, (device >> 3) & 3, device & 7
+    return devices - 1 - ((((y + 1) & 3) << 5) | (((x + 1) & 3) << 3) | ((z * 3) & 7))
 
 
 def chunk_slot(slot, devices):

time: 91.1 us -> 88.9 us (0.976)
  blocking collectives: 83.3 us -> 81.7 us
    all_to_all x2, blocking collectives: 83.3 us -> 81.7 us  [exchange(): lax.all_to_all(x, 'dev', split_axis=0, concat_axis=0, axis_index_groups=[...]
where the time goes in v8:
time: 88.9 us; the launch traced here: 88.7 us
  blocking collectives  81.7 us (92%)
  Pallas kernels  6.43 us (7%)
    all_to_all x2, blocking collectives, exchange(): lax.all_to_all(x, 'dev', split_axis=0, concat_axis=0, axis_index_groups=[...  81.7 us
    pallas_call x1, Pallas kernels, body(): pl.pallas_call(place_kernel, out_shape=(jax.ShapeDtypeStruct((devices, ti...  3.76 us
    pallas_call x1, Pallas kernels, body(): pl.pallas_call(best_kernel, out_shape=(jax.ShapeDtypeStruct((devices, LAN...  2.05 us

profile of v8, /device:TPU:2, one launch (start us, length us, event | category | flops | bytes accessed | tf_op | source)
XLA Modules:
  0.0 88.7 jit_solution(11221737729004234988)
XLA Ops:
  0.6 3.8 %place.1 = (bf16[128,33,2,128]{3,2,1,0:T(2,128)(2,1)S(1)}, s32[1,128]{1,0:T(1,128)S(1)}, s32[1,128]{1,0:T(1,128)S(1)}) custom-call(f32[128,4096]{1,0:T(8,128)} %emb_ref.1, s32[1,128]{1,0:T(1,128)} %bitcast.15, s32[1,128]{1,0:T(1,128)} %bitcast.16, s32[1,256]{1,0:T(1,128)} %bitcast.13, s32[1,256]{1,0:T(1,128)} %bitcast.14), custom_call_target="tpu_custom_call" | custom-call | tf_op jit(solution)/shard_map/place/pallas_call | solution.py:161
  4.4 63.7 %all_to_all.10.got_ref = bf16[128,33,2,128]{3,2,1,0:T(2,128)(2,1)S(1)} all-to-all(bf16[128,33,2,128]{3,2,1,0:T(2,128)(2,1)S(1)} %get-tuple-element.10), channel_id=1, replica_groups={{170,164,174,168,162,172,166,160,154,148,158,152,146,156,150,144,138,13..., dimensions={0} | all-to-all | bytes 4325376 | tf_op jit(solution)/shard_map/all_to_all | solution.py:40
  68.1 2.0 %best.1 = (f32[128,128]{1,0:T(8,128)S(1)}, f32[1,2]{1,0:T(1,128)}) custom-call(bf16[128,33,2,128]{3,2,1,0:T(2,128)(2,1)S(1)} %all_to_all.10.got_ref, s32[1,128]{1,0:T(1,128)S(1)} %get-tuple-element.11.own_ref), custom_call_target="tpu_custom_call" | custom-call | tf_op jit(solution)/shard_map/best/pallas_call | solution.py:182
  70.1 18.0 %all_to_all.11 = f32[128,1,128]{2,1,0:T(1,128)S(1)} all-to-all(f32[128,1,128]{2,1,0:T(1,128)S(1)} %bitcast.12), channel_id=1, replica_groups={{170,164,174,168,162,172,166,160,154,148,158,152,146,156,150,144,138,13..., dimensions={0} | all-to-all | bytes 131072 | tf_op jit(solution)/shard_map/all_to_all | solution.py:40
  88.1 0.6 pick.1

commit v9 on v7

--- a/solution.py
+++ b/solution.py
@@ -27,7 +27,9 @@
 
 
 def chunk_of(device, devices):
-    return devices - 1 - device
+    y, x, z = ((device >> 5) + 1) & 3, ((device >> 3) + 1) & 3, (device * 3) & 7
+    y, x = ((y & 1) << 1) | (y >> 1), ((x & 1) << 1) | (x >> 1)
+    return devices - 1 - ((y << 5) | (x << 3) | z)
 
 
 def chunk_slot(slot, devices):

time: 91.1 us -> 88.1 us (0.967)
  blocking collectives: 83.3 us -> 80.9 us
    all_to_all x2, blocking collectives: 83.3 us -> 80.9 us  [exchange(): lax.all_to_all(x, 'dev', split_axis=0, concat_axis=0, axis_index_groups=[...]
where the time goes in v9:
time: 88.1 us; the launch traced here: 88 us
  blocking collectives  80.9 us (92%)
  Pallas kernels  6.43 us (7%)
    all_to_all x2, blocking collectives, exchange(): lax.all_to_all(x, 'dev', split_axis=0, concat_axis=0, axis_index_groups=[...  80.9 us
    pallas_call x1, Pallas kernels, body(): pl.pallas_call(place_kernel, out_shape=(jax.ShapeDtypeStruct((devices, ti...  3.76 us
    pallas_call x1, Pallas kernels, body(): pl.pallas_call(best_kernel, out_shape=(jax.ShapeDtypeStruct((devices, LAN...  2.04 us

profile of v9, /device:TPU:2, one launch (start us, length us, event | category | flops | bytes accessed | tf_op | source)
XLA Modules:
  0.0 88.0 jit_solution(17081622279024534548)
XLA Ops:
  0.6 3.8 %place.1 = (bf16[128,33,2,128]{3,2,1,0:T(2,128)(2,1)S(1)}, s32[1,128]{1,0:T(1,128)S(1)}, s32[1,128]{1,0:T(1,128)S(1)}) custom-call(f32[128,4096]{1,0:T(8,128)} %emb_ref.1, s32[1,128]{1,0:T(1,128)} %bitcast.15, s32[1,128]{1,0:T(1,128)} %bitcast.16, s32[1,256]{1,0:T(1,128)} %bitcast.13, s32[1,256]{1,0:T(1,128)} %bitcast.14), custom_call_target="tpu_custom_call" | custom-call | tf_op jit(solution)/shard_map/place/pallas_call | solution.py:162
  4.4 63.3 %all_to_all.10.got_ref = bf16[128,33,2,128]{3,2,1,0:T(2,128)(2,1)S(1)} all-to-all(bf16[128,33,2,128]{3,2,1,0:T(2,128)(2,1)S(1)} %get-tuple-element.10), channel_id=1, replica_groups={{170,164,174,168,162,172,166,160,138,132,142,136,130,140,134,128,154,14..., dimensions={0} | all-to-all | bytes 4325376 | tf_op jit(solution)/shard_map/all_to_all | solution.py:41
  67.7 2.0 %best.1 = (f32[128,128]{1,0:T(8,128)S(1)}, f32[1,2]{1,0:T(1,128)}) custom-call(bf16[128,33,2,128]{3,2,1,0:T(2,128)(2,1)S(1)} %all_to_all.10.got_ref, s32[1,128]{1,0:T(1,128)S(1)} %get-tuple-element.11.own_ref), custom_call_target="tpu_custom_call" | custom-call | tf_op jit(solution)/shard_map/best/pallas_call | solution.py:183
  69.7 17.6 %all_to_all.11 = f32[128,1,128]{2,1,0:T(1,128)S(1)} all-to-all(f32[128,1,128]{2,1,0:T(1,128)S(1)} %bitcast.12), channel_id=1, replica_groups={{170,164,174,168,162,172,166,160,138,132,142,136,130,140,134,128,154,14..., dimensions={0} | all-to-all | bytes 131072 | tf_op jit(solution)/shard_map/all_to_all | solution.py:41
  87.3 0.6 pick.1

commit v10 on v9

--- a/solution.py
+++ b/solution.py
@@ -29,7 +29,7 @@
 def chunk_of(device, devices):
     y, x, z = ((device >> 5) + 1) & 3, ((device >> 3) + 1) & 3, (device * 3) & 7
     y, x = ((y & 1) << 1) | (y >> 1), ((x & 1) << 1) | (x >> 1)
-    return devices - 1 - ((y << 5) | (x << 3) | z)
+    return devices - 1 - ((z << 4) | (y << 2) | x)
 
 
 def chunk_slot(slot, devices):

time: 88.1 us -> 89 us (1.010)
  no operation moved by 1% of the time
where the time goes in v10:
time: 89 us; the launch traced here: 88.7 us
  blocking collectives  81.7 us (92%)
  Pallas kernels  6.43 us (7%)
    all_to_all x2, blocking collectives, exchange(): lax.all_to_all(x, 'dev', split_axis=0, concat_axis=0, axis_index_groups=[...  81.7 us
    pallas_call x1, Pallas kernels, body(): pl.pallas_call(place_kernel, out_shape=(jax.ShapeDtypeStruct((devices, ti...  3.76 us
    pallas_call x1, Pallas kernels, body(): pl.pallas_call(best_kernel, out_shape=(jax.ShapeDtypeStruct((devices, LAN...  2.04 us

profile of v10, /device:TPU:2, one launch (start us, length us, event | category | flops | bytes accessed | tf_op | source)
XLA Modules:
  0.0 88.7 jit_solution(17301110061006902033)
XLA Ops:
  0.6 3.8 %place.1 = (bf16[128,33,2,128]{3,2,1,0:T(2,128)(2,1)S(1)}, s32[1,128]{1,0:T(1,128)S(1)}, s32[1,128]{1,0:T(1,128)S(1)}) custom-call(f32[128,4096]{1,0:T(8,128)} %emb_ref.1, s32[1,128]{1,0:T(1,128)} %bitcast.15, s32[1,128]{1,0:T(1,128)} %bitcast.16, s32[1,256]{1,0:T(1,128)} %bitcast.13, s32[1,256]{1,0:T(1,128)} %bitcast.14), custom_call_target="tpu_custom_call" | custom-call | tf_op jit(solution)/shard_map/place/pallas_call | solution.py:162
  4.4 62.6 %all_to_all.10.got_ref = bf16[128,33,2,128]{3,2,1,0:T(2,128)(2,1)S(1)} all-to-all(bf16[128,33,2,128]{3,2,1,0:T(2,128)(2,1)S(1)} %get-tuple-element.10), channel_id=1, replica_groups={{170,138,154,186,42,10,26,58,106,74,90,122,234,202,218,250,164,132,148,..., dimensions={0} | all-to-all | bytes 4325376 | tf_op jit(solution)/shard_map/all_to_all | solution.py:41
  67.0 2.0 %best.1 = (f32[128,128]{1,0:T(8,128)S(1)}, f32[1,2]{1,0:T(1,128)}) custom-call(bf16[128,33,2,128]{3,2,1,0:T(2,128)(2,1)S(1)} %all_to_all.10.got_ref, s32[1,128]{1,0:T(1,128)S(1)} %get-tuple-element.11.own_ref), custom_call_target="tpu_custom_call" | custom-call | tf_op jit(solution)/shard_map/best/pallas_call | solution.py:183
  69.1 19.0 %all_to_all.11 = f32[128,1,128]{2,1,0:T(1,128)S(1)} all-to-all(f32[128,1,128]{2,1,0:T(1,128)S(1)} %bitcast.12), channel_id=1, replica_groups={{170,138,154,186,42,10,26,58,106,74,90,122,234,202,218,250,164,132,148,..., dimensions={0} | all-to-all | bytes 131072 | tf_op jit(solution)/shard_map/all_to_all | solution.py:41
  88.1 0.6 pick.1

commit v11 on v10

--- a/solution.py
+++ b/solution.py
@@ -29,7 +29,7 @@
 def chunk_of(device, devices):
     y, x, z = ((device >> 5) + 1) & 3, ((device >> 3) + 1) & 3, (device * 3) & 7
     y, x = ((y & 1) << 1) | (y >> 1), ((x & 1) << 1) | (x >> 1)
-    return devices - 1 - ((z << 4) | (y << 2) | x)
+    return devices - 1 - ((y << 5) | (z << 2) | x)
 
 
 def chunk_slot(slot, devices):

time: 89 us -> 89.2 us (level)
  no operation moved by 1% of the time
where the time goes in v11:
time: 89.2 us; the launch traced here: 88.7 us
  blocking collectives  81.7 us (92%)
  Pallas kernels  6.43 us (7%)
    all_to_all x2, blocking collectives, exchange(): lax.all_to_all(x, 'dev', split_axis=0, concat_axis=0, axis_index_groups=[...  81.7 us
    pallas_call x1, Pallas kernels, body(): pl.pallas_call(place_kernel, out_shape=(jax.ShapeDtypeStruct((devices, ti...  3.76 us
    pallas_call x1, Pallas kernels, body(): pl.pallas_call(best_kernel, out_shape=(jax.ShapeDtypeStruct((devices, LAN...  2.04 us

profile of v11, /device:TPU:2, one launch (start us, length us, event | category | flops | bytes accessed | tf_op | source)
XLA Modules:
  0.0 88.7 jit_solution(16037861201578111615)
XLA Ops:
  0.6 3.8 %place.1 = (bf16[128,33,2,128]{3,2,1,0:T(2,128)(2,1)S(1)}, s32[1,128]{1,0:T(1,128)S(1)}, s32[1,128]{1,0:T(1,128)S(1)}) custom-call(f32[128,4096]{1,0:T(8,128)} %emb_ref.1, s32[1,128]{1,0:T(1,128)} %bitcast.15, s32[1,128]{1,0:T(1,128)} %bitcast.16, s32[1,256]{1,0:T(1,128)} %bitcast.13, s32[1,256]{1,0:T(1,128)} %bitcast.14), custom_call_target="tpu_custom_call" | custom-call | tf_op jit(solution)/shard_map/place/pallas_call | solution.py:162
  4.4 63.1 %all_to_all.10.got_ref = bf16[128,33,2,128]{3,2,1,0:T(2,128)(2,1)S(1)} all-to-all(bf16[128,33,2,128]{3,2,1,0:T(2,128)(2,1)S(1)} %get-tuple-element.10), channel_id=1, replica_groups={{170,138,154,186,164,132,148,180,174,142,158,190,168,136,152,184,162,13..., dimensions={0} | all-to-all | bytes 4325376 | tf_op jit(solution)/shard_map/all_to_all | solution.py:41
  67.5 2.0 %best.1 = (f32[128,128]{1,0:T(8,128)S(1)}, f32[1,2]{1,0:T(1,128)}) custom-call(bf16[128,33,2,128]{3,2,1,0:T(2,128)(2,1)S(1)} %all_to_all.10.got_ref, s32[1,128]{1,0:T(1,128)S(1)} %get-tuple-element.11.own_ref), custom_call_target="tpu_custom_call" | custom-call | tf_op jit(solution)/shard_map/best/pallas_call | solution.py:183
  69.5 18.6 %all_to_all.11 = f32[128,1,128]{2,1,0:T(1,128)S(1)} all-to-all(f32[128,1,128]{2,1,0:T(1,128)S(1)} %bitcast.12), channel_id=1, replica_groups={{170,138,154,186,164,132,148,180,174,142,158,190,168,136,152,184,162,13..., dimensions={0} | all-to-all | bytes 131072 | tf_op jit(solution)/shard_map/all_to_all | solution.py:41
  88.1 0.6 pick.1
